TPU v7x, 128 devices: a whole 4x4x4 slice. The times are simulated.
128 devices in a mesh: expert: 16 (over y, x_hi, core), dp: 8 (over x_lo, z).
Axes of the slice: x: 4 (x_hi: 2, x_lo: 2; x = x_hi * 2 + x_lo), y: 4, z: 4, core: 2. Of those that a mesh axis runs over, the one named last changes fastest.
Arguments:
- gradient: bfloat16 [8, 1, 14336, 2048], P('dp', None, None, 'expert'), may hold values from -6 to 6
- momentum: float32 [8, 1, 14336, 2048], P('dp', None, 'expert'), may hold values from -6 to 6
- group_index: int32 [224, 32, 8, 32], P('expert'), may hold values from 0 to 4095, all different within a row
Outputs:
- momentum_next: float32 [8, 1, 14336, 2048], P('dp', None, 'expert')
- update: float32 [1, 14336, 2048], P(None, None, 'expert')
Inputs may be any that keep to these rules, and one draw needn't show every extreme that they name: `group_index`: an entry names the coefficient at row frequency (entry // 64) and column frequency (entry % 64) of its block; the 32 entries of one block and replica differ.
All inputs are finite; a program needn't handle non-finite values.
Results may differ from a plain program's by a relative error of at most 0.0003.
Values may be sent and summed in bfloat16 or wider, within the bound.
A program may use at most 192 MiB of HBM per device.

v0:
```python
import math

import jax
import jax.numpy as jnp
from jax import lax
from jax.sharding import PartitionSpec as P

SPAN = 64


MOMENTUM_DECAY = 0.999
HIGHEST_PRECISION = lax.Precision.HIGHEST


def in_blocks(x, dim, count):
    before, after = (x.shape[:dim], x.shape[dim + 1 :])
    return jnp.moveaxis(x.reshape(*before, count, -1, *after), dim, 0)


def edges_of(length, count):
    unit = 8 if length >= 8 * count else 1
    return [length // unit * k // count * unit for k in range(1, count)]


def in_order(tiles, dim):
    shape = list(tiles.shape[1:])
    shape[dim] *= tiles.shape[0]
    return jnp.moveaxis(tiles, 0, dim).reshape(shape)


def several_exchanges(x, axis, pieces, split_dim, concat_dim):
    tiles = in_blocks(x, split_dim, lax.axis_size(axis))
    split_at = max(range(1, max(2, tiles.ndim - 1)), key=lambda d: tiles.shape[d])
    outs = []
    for piece in jnp.split(tiles, edges_of(tiles.shape[split_at], pieces), axis=split_at):
        if piece.size:
            outs.append(lax.all_to_all(piece, axis, split_axis=0, concat_axis=0, tiled=True))
    return in_order(jnp.concatenate(outs, axis=split_at), concat_dim)


def cosine_table(order_size):
    frequency = jnp.arange(order_size, dtype=jnp.float32)[:, None]
    position = jnp.arange(order_size, dtype=jnp.float32)[None, :]
    weighting = jnp.where(frequency == 0, math.sqrt(1.0 / order_size), math.sqrt(2.0 / order_size))
    return weighting * jnp.cos(math.pi * (2.0 * position + 1.0) * frequency / (2.0 * order_size))


def forward(blocks, cosine):
    return jnp.einsum("ui,piqj,vj->pquv", cosine, blocks, cosine, precision=HIGHEST_PRECISION)


def inverse(coeffs, cosine):
    return jnp.einsum("ui,pquv,vj->piqj", cosine, coeffs, cosine, precision=HIGHEST_PRECISION)


def place(values, picked, total):
    count_rows = picked.shape[0]
    count_cols = picked.shape[1]
    row_ids = jnp.arange(count_rows, dtype=jnp.int32)[:, None, None]
    col_ids = jnp.arange(count_cols, dtype=jnp.int32)[None, :, None]
    empty = jnp.zeros((count_rows, count_cols, total), jnp.float32)
    return empty.at[row_ids, col_ids, picked].add(values)


def on_device(gradient, momentum, group_index):
    cosine = cosine_table(SPAN)
    replica = lax.axis_index("dp")
    shifted = several_exchanges(gradient, "expert", 2, 2, 3)
    row_count = shifted.shape[1] * shifted.shape[2]
    col_count = shifted.shape[3]
    decayed = MOMENTUM_DECAY * momentum.reshape(row_count, col_count) + shifted.reshape(
        row_count, col_count
    ).astype(jnp.float32)
    block_rows = row_count // SPAN
    block_cols = col_count // SPAN
    blocks = decayed.reshape(block_rows, SPAN, block_cols, SPAN)
    coeffs = forward(blocks, cosine).reshape(block_rows, block_cols, SPAN * SPAN)
    own = lax.dynamic_index_in_dim(group_index, replica, 2, keepdims=False)
    values = jnp.take_along_axis(coeffs, own, axis=2)
    selected = place(values, own, SPAN * SPAN).reshape(block_rows, block_cols, SPAN, SPAN)
    restored = inverse(selected, cosine).reshape(row_count, col_count)
    momentum_next = (decayed - restored).reshape(momentum.shape)
    total = lax.psum(restored, "dp")
    update = several_exchanges(total[None], "expert", 2, 2, 1)
    return (momentum_next, update)


def solution(mesh):
    placed = (
        P("dp", None, None, "expert"),
        P("dp", None, "expert", None),
        P("expert", None, None, None),
    )
    return jax.shard_map(
        on_device,
        mesh=mesh,
        in_specs=placed,
        out_specs=(P("dp", None, "expert", None), P(None, None, "expert")),
        check_vma=False,
    )
```

profile of v0, /device:TPU:1, one launch (start us, length us, event | category | flops | bytes accessed | tf_op | source)
XLA Modules:
  0.0 818.2 jit_solution(18265335012599855802)
XLA Ops:
  7.2 0.0 copy-start
  7.2 4.3 fusion.28
  11.5 8.4 %all-to-all-start = ((bf16[16,1,1,448,128]{4,3,2,1,0:T(8,128)(2,1)}), bf16[16,1,1,448,128]{4,3,2,1,0:T(8,128)(2,1)}, u32[]{:S(2)}, u32[]{:S(2)}) async-start(bf16[16,1,1,448,128]{4,3,2,1,0:T(8,128)(2,1)} %get-tuple-element.6), calls=%async_computation | async-start | bytes 3670016 | tf_op jit(solution)/shard_map/all_to_all | solution.py:37
  19.9 25.6 %all-to-all-done = bf16[16,1,1,448,128]{4,3,2,1,0:T(8,128)(2,1)} async-done(((bf16[16,1,1,448,128]{4,3,2,1,0:T(8,128)(2,1)}), bf16[16,1,1,448,128]{4,3,2,1,0:T(8,128)(2,1)}, u32[]{:S(2)}, u32[]{:S(2)}) %all-to-all-start) | async-done | bytes 1835040 | tf_op jit(solution)/shard_map/all_to_all | solution.py:37
  45.5 5.2 all-to-all-start.1
  50.7 0.0 all-reduce.2.cloned.1.call-start
  50.8 7.7 broadcast_multiply_fusion
  58.5 0.0 copy-start.3
  58.5 0.0 copy-start.2
  58.5 12.7 %mul.98 = f32[14,64,32,64]{3,2,1,0:T(8,128)} reshape(f32[1,1,896,2048]{3,2,1,0:T(8,128)} %broadcast_multiply_fusion) | data formatting | bytes 14680064 | tf_op jit(solution)/shard_map/mul | solution.py:71
  71.2 0.0 copy-done
  71.2 0.2 constant_dynamic-slice_fusion
  71.4 0.1 shift-left_or_fusion
  71.5 0.1 reshape.107
  71.7 0.0 copy-done.3
  71.7 0.1 multiply_reduce_fusion
  71.8 0.0 copy-done.2
  71.8 0.2 and_reduce_fusion
  72.1 0.1 reshape.113
  72.2 4.2 all-to-all-done.1
  76.5 6.1 convert_bitcast_fusion
  82.5 7.3 copy.28
  89.8 11.4 %reshape.106 = f32[14,64,32,64]{3,2,1,0:T(8,128)} reshape(f32[1,1,896,16,128]{4,3,2,1,0:T(8,128)} %copy.28) | data formatting | bytes 14680064 | tf_op jit(solution)/shard_map/convert_element_type | solution.py:73
  101.2 15.0 %add.64 = f32[14,64,32,64]{3,2,1,0:T(8,128)} add(f32[14,64,32,64]{3,2,1,0:T(8,128)} %mul.98, f32[14,64,32,64]{3,2,1,0:T(8,128)} %reshape.106) | non-fusion elementwise | flops 1835008 | bytes 22020096 | tf_op jit(solution)/shard_map/add | solution.py:71
  116.2 27.7 %fusion = f32[14,32,64,64]{2,3,1,0:T(8,128)S(1)} fusion(f32[14,64,32,64]{3,2,1,0:T(8,128)} %add.64, f32[64]{0:T(128)S(1)} %get-tuple-element.11, f32[64]{0:T(128)S(1)} %get-tuple-element.10), kind=kOutput, calls=%fused_computation.2 | convolution fusion | flops 1409298432 | bytes 14680576 | tf_op jit(solution)/shard_map/ui,piqj,vj->pquv/dot_general | solution.py:49
  143.9 14.9 %fusion.8 = f32[14,32,64,64]{3,2,1,0:T(8,128)} fusion(f32[14,32,64,64]{2,3,1,0:T(8,128)S(1)} %fusion, f32[64]{0:T(128)S(1)} %get-tuple-element.11, f32[64]{0:T(128)S(1)} %get-tuple-element.10), kind=kOutput, calls=%fused_computation.25 | convolution fusion | flops 1409298432 | bytes 14680576 | tf_op jit(solution)/shard_map/ui,piqj,vj->pquv/dot_general | solution.py:49
  158.8 12.9 %reshape.95 = f32[14,32,4096]{2,1,0:T(8,128)} reshape(f32[14,32,64,64]{3,2,1,0:T(8,128)} %fusion.8) | data formatting | bytes 14680064 | tf_op jit(solution)/shard_map/reshape | solution.py:77
  171.7 199.8 %gather_fusion = f32[14336]{0:T(1024)S(1)} fusion(f32[14,32,4096]{2,1,0:T(8,128)} %reshape.95, s32[14336]{0:T(1024)S(1)} %reshape.107), kind=kCustom, calls=%fused_computation | custom fusion | bytes 286720 | tf_op jit(solution)/shard_map/jit(take_along_axis)/gather | solution.py:79
  371.5 0.1 reshape.110
  371.6 0.1 and_select_fusion
  371.7 0.1 reshape.115
  371.8 78.6 %scatter_custom_fusion = f32[1835008]{0:T(1024)} fusion(s32[14336]{0:T(1024)S(1)} %reshape.113, f32[14336]{0:T(1024)S(1)} %reshape.115, f32[]{:T(128)} %constant.15.clone.1), kind=kCustom, calls=%fused_computation.11 | custom fusion | flops 14336 | bytes 7340036
  450.4 11.5 %reshape.96 = f32[14,32,64,64]{3,2,1,0:T(8,128)} reshape(f32[1835008]{0:T(1024)} %scatter_custom_fusion) | data formatting | bytes 14680064 | tf_op jit(solution)/shard_map/reshape | solution.py:80
  462.0 18.2 %fusion.6 = f32[14,32,64,64]{2,3,1,0:T(8,128)S(1)} fusion(f32[14,32,64,64]{3,2,1,0:T(8,128)} %reshape.96, f32[64]{0:T(128)S(1)} %get-tuple-element.11, f32[64]{0:T(128)S(1)} %get-tuple-element.10), kind=kOutput, calls=%fused_computation.23 | convolution fusion | flops 1409298432 | bytes 14680576 | tf_op jit(solution)/shard_map/ui,pquv,vj->piqj/dot_general | solution.py:53
  480.2 14.7 %convolution_bitcast_fusion = f32[14,64,32,64]{3,1,2,0:T(8,128)} fusion(f32[14,32,64,64]{2,3,1,0:T(8,128)S(1)} %fusion.6, f32[64]{0:T(128)S(1)} %get-tuple-element.11, f32[64]{0:T(128)S(1)} %get-tuple-element.10), kind=kOutput, calls=%fused_computation.6 | convolution fusion | flops 1409298432 | bytes 14680576 | tf_op jit(solution)/shard_map/ui,pquv,vj->piqj/dot_general | solution.py:53
  494.8 21.3 %copy.34 = f32[14,64,32,64]{3,2,1,0:T(8,128)} copy(f32[14,64,32,64]{3,1,2,0:T(8,128)} %convolution_bitcast_fusion) | data formatting | bytes 14680064 | tf_op jit(solution)/shard_map/ui,pquv,vj->piqj/transpose | solution.py:53
  516.1 12.8 %reshape_broadcast_in_dim.3 = f32[1,896,16,128]{3,2,1,0:T(8,128)} reshape(f32[14,64,32,64]{3,2,1,0:T(8,128)} %copy.34) | data formatting | bytes 14680064 | tf_op jit(solution)/shard_map/reshape;broadcast_in_dim | solution.py:17
  529.0 0.0 all-reduce.2.cloned.1.call-update
  529.0 163.3 %all-reduce.2.cloned.1.call-done = f32[16,1,896,128]{3,0,2,1:T(8,128)} async-done(((f32[16,1,896,128]{3,0,2,1:T(8,128)}), f32[16,1,896,128]{3,0,2,1:T(8,128)}) %all-reduce.2.cloned.1.call-update) | async-done | bytes 7340048 | tf_op jit(solution)/shard_map/psum | solution.py:83
  692.3 5.5 fusion.27
  697.7 2.9 copy.36
  700.7 7.3 all-to-all-start.2
  708.0 5.1 copy.37
  713.0 40.2 %all-to-all-done.2 = f32[16,1,448,128]{3,2,1,0:T(8,128)} async-done(((f32[16,1,448,128]{3,2,1,0:T(8,128)}), f32[16,1,448,128]{3,2,1,0:T(8,128)}, u32[]{:S(2)}, u32[]{:S(2)}) %all-to-all-start.2) | async-done | bytes 3670048 | tf_op jit(solution)/shard_map/all_to_all | solution.py:37
  753.3 5.3 all-to-all-start.3
  758.5 13.2 %reshape.97 = f32[1,1,896,2048]{3,2,1,0:T(8,128)} reshape(f32[14,64,32,64]{3,2,1,0:T(8,128)} %copy.34) | data formatting | bytes 14680064 | tf_op jit(solution)/shard_map/reshape | solution.py:81
  771.8 13.0 %fusion.2 = f32[1,1,896,2048]{3,2,1,0:T(8,128)} fusion(f32[1,1,896,2048]{3,2,1,0:T(8,128)} %reshape.97, f32[16,1,1,112,8,128]{5,4,3,2,1,0:T(8,128)} %get-tuple-element.4, f32[1,1,896,2048]{3,2,1,0:T(8,128)} %param.4), kind=kLoop, calls=%fused_computation.8 | loop fusion | flops 5505024 | bytes 29360128 | tf_op jit(solution)/shard_map/sub | solution.py:82
  784.7 19.2 %all-to-all-done.3 = f32[16,1,448,128]{3,2,1,0:T(8,128)} async-done(((f32[16,1,448,128]{3,2,1,0:T(8,128)}), f32[16,1,448,128]{3,2,1,0:T(8,128)}, u32[]{:S(2)}, u32[]{:S(2)}) %all-to-all-start.3) | async-done | bytes 3670048 | tf_op jit(solution)/shard_map/all_to_all | solution.py:37
  803.9 0.0 copy-start.1
  803.9 7.0 pad_maximum_fusion
  810.9 0.0 copy-done.1
  (4 shorter events, 0.1 us)
Async XLA Ops:
  7.2 64.0 %copy-start = (s32[14,32,8,32]{3,2,1,0:T(8,128)S(1)}, s32[14,32,8,32]{3,2,1,0:T(8,128)}, u32[]{:S(2)}) copy-start(s32[14,32,8,32]{3,2,1,0:T(8,128)} %param.5) | copy-start | bytes 1376260
  11.5 34.1 %all-to-all-start = ((bf16[16,1,1,448,128]{4,3,2,1,0:T(8,128)(2,1)}), bf16[16,1,1,448,128]{4,3,2,1,0:T(8,128)(2,1)}, u32[]{:S(2)}, u32[]{:S(2)}) async-start(bf16[16,1,1,448,128]{4,3,2,1,0:T(8,128)(2,1)} %get-tuple-element.6), calls=%async_computation | async-start | bytes 3670016 | tf_op jit(solution)/shard_map/all_to_all | solution.py:37
  45.5 30.9 %all-to-all-start.1 = ((bf16[16,1,1,448,128]{4,3,2,1,0:T(8,128)(2,1)}), bf16[16,1,1,448,128]{4,3,2,1,0:T(8,128)(2,1)}, u32[]{:S(2)}, u32[]{:S(2)}) async-start(bf16[16,1,1,448,128]{4,3,2,1,0:T(8,128)(2,1)} %get-tuple-element.7), calls=%async_computation.1 | async-start | bytes 3670016 | tf_op jit(solution)/shard_map/all_to_all | solution.py:37
  50.7 641.6 %all-reduce.2.cloned.1.call-start = ((), (), s32[]{:S(2)}) async-start(), calls=%async_computation.4 | async-start | bytes 14680064 | tf_op jit(solution)/shard_map/psum | solution.py:83
  58.5 13.2 %copy-start.3 = (s32[3]{0:T(128)S(1)}, s32[3]{0:T(128)}, u32[]{:S(2)}) copy-start(s32[3]{0:T(128)} %constant.54) | copy-start | bytes 40
  58.5 13.3 %copy-start.2 = (s32[3]{0:T(128)S(1)}, s32[3]{0:T(128)}, u32[]{:S(2)}) copy-start(s32[3]{0:T(128)} %constant.57) | copy-start | bytes 40
  700.7 52.6 %all-to-all-start.2 = ((f32[16,1,448,128]{3,2,1,0:T(8,128)}), f32[16,1,448,128]{3,2,1,0:T(8,128)}, u32[]{:S(2)}, u32[]{:S(2)}) async-start(f32[16,1,448,128]{3,2,1,0:T(8,128)} %copy.36), calls=%async_computation.2 | async-start | bytes 7340032 | tf_op jit(solution)/shard_map/all_to_all | solution.py:37
  753.3 50.7 %all-to-all-start.3 = ((f32[16,1,448,128]{3,2,1,0:T(8,128)}), f32[16,1,448,128]{3,2,1,0:T(8,128)}, u32[]{:S(2)}, u32[]{:S(2)}) async-start(f32[16,1,448,128]{3,2,1,0:T(8,128)} %copy.37), calls=%async_computation.3 | async-start | bytes 7340032 | tf_op jit(solution)/shard_map/all_to_all | solution.py:37
  803.9 7.0 copy-start.1
Sparse Core Ops, SparseCore 0:
  529.1 163.1 all-reduce.1
where the time goes:
time: 834 us; the launch traced here: 818 us
  local copies, waits for them, and re-layouts  321 us (38%)
  waiting for transfers between devices  253 us (30%)
  other arithmetic  128 us (15%)
  matrix products  75.5 us (9%)
  starting transfers between devices  26.2 us (3%)
  between operations  14.6 us (2%)
    gather x2, local copies, waits for them, and re-layouts, on_device(): values = jnp.take_along_axis(coeffs, own, axis=2)  200 us
    psum x1, waiting for transfers between devices, on_device(): total = lax.psum(restored, 'dp')  163 us
    all_to_all x4, waiting for transfers between devices, several_exchanges(): lax.all_to_all(piece, axis, split_axis=0, concat_axis=0, tiled=True)  89.3 us
    unnamed x5, other arithmetic  85.1 us
    dot_general x2, matrix products, forward(): jnp.einsum('ui,piqj,vj->pquv', cosine, blocks, cosine, precision=HIGHEST_...  42.6 us
    dot_general x2, matrix products, inverse(): jnp.einsum('ui,pquv,vj->piqj', cosine, coeffs, cosine, precision=HIGHEST_...  32.9 us
    all_to_all x4, starting transfers between devices, several_exchanges(): lax.all_to_all(piece, axis, split_axis=0, concat_axis=0, tiled=True)  26.1 us
    transpose x1, local copies, waits for them, and re-layouts, inverse(): jnp.einsum('ui,pquv,vj->piqj', cosine, coeffs, cosine, precision=HIGHEST_...  21.3 us
  transfers between devices with their start and end apart: 5, of which 5 were waited for; matrix products, arithmetic and copies ran while one was open for 6% of the time, Pallas kernels for 0%

commit v1 on v0

v1 whole, which is shorter than its diff:
```python
import functools

import jax
import jax.numpy as jnp
import numpy as np
from jax import lax
from jax.experimental import pallas as pl
from jax.experimental.pallas import tpu as pltpu
from jax.sharding import PartitionSpec as P

SPAN = 64
TOPK = 32
DECAY = 0.999
LANES = 128
GROUP = 8

F32 = jnp.float32
BF16 = jnp.bfloat16


def cosine_table():
    u = np.arange(SPAN, dtype=np.float64)[:, None]
    i = np.arange(SPAN, dtype=np.float64)[None, :]
    weight = np.where(u == 0, np.sqrt(1.0 / SPAN), np.sqrt(2.0 / SPAN))
    return weight * np.cos(np.pi * (2.0 * i + 1.0) * u / (2.0 * SPAN))


def two_parts(x):
    high = x.astype(jnp.bfloat16.dtype)
    low = (x - high.astype(np.float64)).astype(jnp.bfloat16.dtype)
    return high, low


def tables():
    c = cosine_table()
    ct_high, ct_low = two_parts(c.T)
    ct = np.concatenate([ct_high, ct_low], axis=0)
    four = np.kron(np.eye(4), c)
    four_high, four_low = two_parts(four)
    return ct, np.stack([four_high, four_low])


def split(x):
    high = x.astype(BF16)
    return high, (x - high.astype(F32)).astype(BF16)


def dot(a, b):
    return jnp.dot(a, b, preferred_element_type=F32)


def dot_nt(a, b):
    return lax.dot_general(a, b, (((1,), (1,)), ((), ())), preferred_element_type=F32)


def values_of(x, picked, ct):
    rows = lax.broadcasted_iota(jnp.int32, (SPAN, LANES), 0)
    owner = lax.broadcasted_iota(jnp.int32, (SPAN, LANES), 1) // TOPK
    at_u = jnp.where(rows == (picked >> 6), 1.0, 0.0).astype(BF16)
    at_v = jnp.where(rows == (picked & 63), 1.0, 0.0).astype(BF16)
    both = dot(ct, jnp.concatenate([at_u, at_v], axis=1))
    left = both[:SPAN, :LANES] + both[SPAN:, :LANES]
    spread = []
    for part in (both[:SPAN, LANES:], both[SPAN:, LANES:]):
        spread.append(
            jnp.concatenate([jnp.where(owner == q, part, 0.0).astype(BF16) for q in range(4)], axis=0)
        )
    right = jnp.concatenate(spread, axis=1)
    if x.dtype == BF16:
        z = dot(x, right)
        z = z[:, :LANES] + z[:, LANES:]
    else:
        high, low = split(x)
        z = dot(jnp.concatenate([high, low], axis=0), right)
        z = z[:SPAN, :LANES] + (z[:SPAN, LANES:] + z[SPAN:, :LANES] + z[SPAN:, LANES:])
    return jnp.sum(left * z, axis=0, keepdims=True)


def inverse(s, ct, four_ref):
    high, low = split(s)
    z = dot(high, four_ref[0]) + (dot(low, four_ref[0]) + dot(high, four_ref[1]))
    high, low = split(z)
    y = dot(ct, high)
    return y[:SPAN] + (y[SPAN:] + dot(ct[:SPAN], low))


def values_wide_kernel(x_ref, picked_ref, ct_ref, out_ref):
    for n in range(GROUP):
        x = x_ref[:, n * 256 : (n + 1) * 256]
        out_ref[n : n + 1, :] = values_of(x, picked_ref[n : n + 1, :], ct_ref[...])


def values_tall_kernel(x_ref, picked_ref, ct_ref, out_ref):
    for n in range(GROUP):
        x = jnp.concatenate(
            [x_ref[n * 128 : n * 128 + SPAN, :], x_ref[n * 128 + SPAN : n * 128 + 128, :]], axis=1
        )
        out_ref[n : n + 1, :] = values_of(x, picked_ref[n : n + 1, :], ct_ref[...])


def remain_kernel(x_ref, picked_ref, value_ref, ct_ref, four_ref, out_ref):
    rows = lax.broadcasted_iota(jnp.int32, (SPAN, LANES), 0)
    rows4 = lax.broadcasted_iota(jnp.int32, (256, LANES), 0)
    owner = lax.broadcasted_iota(jnp.int32, (1, LANES), 1) // TOPK
    for n in range(GROUP):
        picked = picked_ref[n : n + 1, :]
        value = value_ref[n : n + 1, :]
        high = value.astype(BF16).astype(F32)
        at_u = rows == (picked >> 6)
        left = jnp.concatenate(
            [jnp.where(at_u, high, 0.0).astype(BF16), jnp.where(at_u, value - high, 0.0).astype(BF16)],
            axis=0,
        )
        at_v = jnp.where(rows4 == (owner * SPAN + (picked & 63)), 1.0, 0.0).astype(BF16)
        s = dot_nt(left, at_v)
        restored = inverse(s[:SPAN] + s[SPAN:], ct_ref[...], four_ref)
        here = slice(n * 256, (n + 1) * 256)
        out_ref[:, here] = DECAY * x_ref[:, here] - restored


def update_kernel(picked_ref, value_ref, ct_ref, four_ref, out_ref, s_ref):
    rows = lax.broadcasted_iota(jnp.int32, (SPAN, 256), 0)
    for n in range(GROUP):
        for b in range(4):
            k = n * 4 + b
            picked = picked_ref[k : k + 1, :]
            value = value_ref[k : k + 1, :]
            high = value.astype(BF16).astype(F32)
            at_u = rows == (picked >> 6)
            left = jnp.concatenate(
                [
                    jnp.where(at_u, high, 0.0).astype(BF16),
                    jnp.where(at_u, value - high, 0.0).astype(BF16),
                ],
                axis=0,
            )
            at_v = jnp.where(rows == (picked & 63), 1.0, 0.0).astype(BF16)
            s = dot_nt(left, at_v)
            s_ref[n, :, b * SPAN : (b + 1) * SPAN] = s[:SPAN] + s[SPAN:]
        restored = inverse(s_ref[n], ct_ref[...], four_ref)
        out_ref[n * 128 : n * 128 + SPAN, :] = restored[:, :LANES]
        out_ref[n * 128 + SPAN : n * 128 + 128, :] = restored[:, LANES:]


def whole(shape):
    return pl.BlockSpec(shape, lambda i: (0,) * len(shape))


def params():
    return pltpu.CompilerParams(dimension_semantics=("arbitrary",))


def values_wide(x, picked, ct):
    rows, cols = x.shape
    return pl.pallas_call(
        values_wide_kernel,
        grid=(rows // SPAN,),
        in_specs=[
            pl.BlockSpec((SPAN, cols), lambda i: (i, 0)),
            pl.BlockSpec((GROUP, LANES), lambda i: (i, 0)),
            whole(ct.shape),
        ],
        out_specs=pl.BlockSpec((GROUP, LANES), lambda i: (i, 0)),
        out_shape=jax.ShapeDtypeStruct(picked.shape, F32),
        compiler_params=params(),
        name="values_wide",
    )(x, picked, ct)


def values_tall(x, picked, ct):
    rows, cols = x.shape
    return pl.pallas_call(
        values_tall_kernel,
        grid=(rows // (GROUP * 128),),
        in_specs=[
            pl.BlockSpec((GROUP * 128, cols), lambda i: (i, 0)),
            pl.BlockSpec((GROUP, LANES), lambda i: (i, 0)),
            whole(ct.shape),
        ],
        out_specs=pl.BlockSpec((GROUP, LANES), lambda i: (i, 0)),
        out_shape=jax.ShapeDtypeStruct(picked.shape, F32),
        compiler_params=params(),
        name="values_tall",
    )(x, picked, ct)


def remain(x, picked, value, ct, four):
    rows, cols = x.shape
    return pl.pallas_call(
        remain_kernel,
        grid=(rows // SPAN,),
        in_specs=[
            pl.BlockSpec((SPAN, cols), lambda i: (i, 0)),
            pl.BlockSpec((GROUP, LANES), lambda i: (i, 0)),
            pl.BlockSpec((GROUP, LANES), lambda i: (i, 0)),
            whole(ct.shape),
            whole(four.shape),
        ],
        out_specs=pl.BlockSpec((SPAN, cols), lambda i: (i, 0)),
        out_shape=jax.ShapeDtypeStruct(x.shape, F32),
        compiler_params=params(),
        name="remain",
    )(x, picked, value, ct, four)


def update_of(picked, value, rows, ct, four):
    blocks = picked.shape[0]
    step = GROUP * 4
    return pl.pallas_call(
        update_kernel,
        grid=(blocks // step,),
        in_specs=[
            pl.BlockSpec((step, 256), lambda i: (i, 0)),
            pl.BlockSpec((step, 256), lambda i: (i, 0)),
            whole(ct.shape),
            whole(four.shape),
        ],
        out_specs=pl.BlockSpec((GROUP * 128, LANES), lambda i: (i, 0)),
        out_shape=jax.ShapeDtypeStruct((rows, LANES), F32),
        scratch_shapes=[pltpu.VMEM((GROUP, SPAN, 256), F32)],
        compiler_params=params(),
        name="update",
    )(picked, value, ct, four)


def finish(left, arrived):
    def kernel(a_ref, g_ref, out_ref):
        for e in range(g_ref.shape[0]):
            here = slice(e * LANES, (e + 1) * LANES)
            out_ref[:, here] = a_ref[:, here] + g_ref[e].astype(F32)

    rows, cols = left.shape
    tall = 64
    return pl.pallas_call(
        kernel,
        grid=(rows // tall,),
        in_specs=[
            pl.BlockSpec((tall, cols), lambda i: (i, 0)),
            pl.BlockSpec((arrived.shape[0], tall, LANES), lambda i: (0, i, 0)),
        ],
        out_specs=pl.BlockSpec((tall, cols), lambda i: (i, 0)),
        out_shape=jax.ShapeDtypeStruct(left.shape, F32),
        compiler_params=params(),
        name="finish",
    )(left, arrived)


def on_device(gradient, momentum, group_index):
    ct, four = (jnp.asarray(t) for t in tables())
    ways = lax.axis_size("expert")
    replicas = lax.axis_size("dp")
    replica = lax.axis_index("dp")
    total_rows = gradient.shape[2]
    rows, cols = momentum.shape[2:]
    block_rows, block_cols = rows // SPAN, cols // SPAN
    wide = block_cols // ways

    gradient = gradient.reshape(total_rows, LANES)
    momentum = momentum.reshape(rows, cols)

    parts = group_index.reshape(block_rows, ways, wide, replicas, TOPK).transpose(1, 0, 2, 3, 4)
    columns = lax.all_to_all(parts, "expert", 0, 0, tiled=True)
    columns = columns.reshape(ways * block_rows * wide, replicas, TOPK)
    own_rows = lax.dynamic_index_in_dim(group_index, replica, 2, keepdims=False).reshape(-1, LANES)
    own_cols = lax.dynamic_index_in_dim(columns, replica, 1, keepdims=False).reshape(-1, LANES)

    arrived = lax.all_to_all(gradient.reshape(ways, rows, LANES), "expert", 0, 0, tiled=True)

    from_rows = DECAY * values_wide(momentum, own_rows, ct)
    from_cols = values_tall(gradient, own_cols, ct)
    out_rows = (
        from_rows.reshape(block_rows, ways, wide * TOPK).transpose(1, 0, 2).reshape(ways, 1, -1)
    )
    out_cols = from_cols.reshape(ways, 1, block_rows * wide * TOPK)
    swapped = lax.all_to_all(jnp.concatenate([out_rows, out_cols], axis=1), "expert", 0, 0, tiled=True)
    at_cols = swapped[:, 0].reshape(-1) + from_cols.reshape(-1)
    back = swapped[:, 1].reshape(ways, block_rows, wide * TOPK).transpose(1, 0, 2)
    at_rows = back.reshape(-1, LANES) + from_rows

    everyone = lax.all_gather(at_cols.reshape(-1, TOPK), "dp", axis=1, tiled=False)
    update = update_of(columns.reshape(-1, 256), everyone.reshape(-1, 256), total_rows, ct, four)
    left = remain(momentum, own_rows, at_rows, ct, four)
    momentum_next = finish(left, arrived)
    return momentum_next.reshape(1, 1, rows, cols), update.reshape(1, total_rows, LANES)


def solution(mesh):
    return jax.shard_map(
        on_device,
        mesh=mesh,
        in_specs=(
            P("dp", None, None, "expert"),
            P("dp", None, "expert", None),
            P("expert", None, None, None),
        ),
        out_specs=(P("dp", None, "expert", None), P(None, None, "expert")),
        check_vma=False,
    )
```

time: 834 us -> 252 us (0.30)
  the two profiles are of different devices: /device:TPU:1 before, /device:TPU:4 now
where the time goes in v1:
time: 252 us; the launch traced here: 251 us
  Pallas kernels  140 us (56%)
  blocking collectives  79.3 us (31%)
  starting transfers between devices  14.8 us (6%)
  local copies, waits for them, and re-layouts  13.1 us (5%)
  other arithmetic  3.22 us (1%)
    all_gather x1, blocking collectives, on_device(): lax.all_gather(at_cols.reshape(-1, TOPK), 'dp', axis=1, tiled=False)  67.3 us
    pallas_call x1, Pallas kernels, update_of(): pl.pallas_call(update_kernel, grid=(blocks // step,), in_specs=[pl.BlockS...  53.8 us
    pallas_call x1, Pallas kernels, remain(): pl.pallas_call(remain_kernel, grid=(rows // SPAN,), in_specs=[pl.BlockSpe...  49.7 us
    pallas_call x1, Pallas kernels, values_wide(): pl.pallas_call(values_wide_kernel, grid=(rows // SPAN,), in_specs=[pl.Blo...  12.8 us
    pallas_call x1, Pallas kernels, values_tall(): pl.pallas_call(values_tall_kernel, grid=(rows // (GROUP * 128),), in_spec...  12.1 us
    all_to_all x1, blocking collectives, on_device(): lax.all_to_all(jnp.concatenate([out_rows, out_cols], axis=1), 'expert', 0...  12.1 us
    pallas_call x1, Pallas kernels, finish(): pl.pallas_call(kernel, grid=(rows // tall,), in_specs=[pl.BlockSpec((tall...  11.2 us
    all_to_all x1, starting transfers between devices, on_device(): columns = lax.all_to_all(parts, 'expert', 0, 0, tiled=True)  7.45 us
  transfers between devices with their start and end apart: 2, of which 0 were waited for; matrix products, arithmetic and copies ran while one was open for 3% of the time, Pallas kernels for 46%

profile of v1, /device:TPU:4, one launch (start us, length us, event | category | flops | bytes accessed | tf_op | source)
XLA Modules:
  0.0 251.0 jit_solution(4828995902824596119)
XLA Ops:
  0.6 1.7 copy.25
  2.3 1.6 reshape.88
  3.9 7.4 %all-to-all-start = ((s32[16,1,7168]{2,1,0:T(1,128)}), s32[16,1,7168]{2,1,0:T(1,128)S(1)}, u32[]{:S(2)}, u32[]{:S(2)}) async-start(s32[16,1,7168]{2,1,0:T(1,128)} %reshape.88), calls=%async_computation | async-start | bytes 917504 | tf_op jit(solution)/shard_map/all_to_all | solution.py:262
  11.3 2.2 dynamic-slice_reduce_fusion
  13.5 0.7 reshape.66.picked_ref
  14.2 12.8 %values_wide.1 = f32[112,128]{1,0:T(8,128)} custom-call(f32[896,2048]{1,0:T(8,128)} %bitcast.19, s32[112,128]{1,0:T(8,128)} %reshape.66.picked_ref, bf16[128,64]{1,0:T(8,128)(2,1)} %constant.20.clone.ct_ref), custom_call_target="tpu_custom_call" | custom-call | tf_op jit(solution)/shard_map/values_wide/pallas_call | solution.py:155
  27.1 0.8 broadcast_multiply_fusion
  27.9 0.1 reshape.67
  28.0 0.1 reshape.68
  28.1 0.0 all-to-all-done
  28.1 0.5 broadcast.5
  28.6 1.7 reduce.8
  30.4 0.6 reshape.89
  31.0 0.9 copy.18
  31.9 0.7 reshape.72.picked_ref
  32.7 12.1 %values_tall.1 = f32[112,128]{1,0:T(8,128)} custom-call(bf16[14336,128]{1,0:T(8,128)(2,1)} %bitcast.21, s32[112,128]{1,0:T(8,128)} %reshape.72.picked_ref, bf16[128,64]{1,0:T(8,128)(2,1)} %constant.20.clone.ct_ref), custom_call_target="tpu_custom_call" | custom-call | tf_op jit(solution)/shard_map/values_tall/pallas_call | solution.py:172
  44.8 0.8 reshape.73
  45.7 0.1 copy.19
  45.8 12.1 %all_to_all.15 = f32[16,2,896]{2,1,0:T(2,128)S(1)} all-to-all(f32[16,2,896]{2,1,0:T(2,128)S(1)} %copy.19), channel_id=1, replica_groups=mesh['expert'=16,'dp'=8] {'expert'}, dimensions={0} | all-to-all | bytes 229376 | tf_op jit(solution)/shard_map/all_to_all | solution.py:275
  57.8 0.0 copy-start.1
  57.8 7.4 %all-to-all-start.2 = ((bf16[16,896,128]{2,1,0:T(8,128)(2,1)}), bf16[16,896,128]{2,1,0:T(8,128)(2,1)}, u32[]{:S(2)}, u32[]{:S(2)}) async-start(bf16[16,896,128]{2,1,0:T(8,128)(2,1)} %bitcast.22), calls=%async_computation.2 | async-start | bytes 7340032 | tf_op jit(solution)/shard_map/all_to_all | solution.py:267
  65.2 0.0 copy-done.1
  65.2 0.0 copy-start
  65.2 0.1 reshape.76
  65.3 1.3 reshape_reshape.7.picked_ref
  66.6 0.3 slice_reduce_fusion
  66.9 0.1 reshape_squeeze.6
  67.1 0.1 reshape.74
  67.1 0.1 reshape_squeeze.7
  67.3 0.1 copy.21
  67.4 67.3 %all_gather.3 = f32[448,8,32]{0,2,1:T(8,128)S(1)} all-gather(f32[448,1,32]{0,2,1:T(8,128)S(1)} %copy.21), channel_id=1, replica_groups=mesh['expert'=16,'dp'=8] {'dp'}, dimensions={1}, use_global_device_ids=true | all-gather | bytes 516096 | tf_op jit(solution)/shard_map/all_gather | solution.py:280
  134.7 1.0 copy.22.value_ref
  135.6 0.0 copy-done
  135.6 0.6 fusion.value_ref
  136.3 49.7 %remain.1.a_ref = f32[896,2048]{1,0:T(8,128)} custom-call(f32[896,2048]{1,0:T(8,128)} %bitcast.20, s32[112,128]{1,0:T(8,128)} %reshape.66.picked_ref, f32[112,128]{1,0:T(8,128)} %fusion.value_ref, bf16[128,64]{1,0:T(8,128)(2,1)} %constant.20.clone.ct_ref, bf16[2,256,256]{2,1,0:T(8,128)(2,1)} %constant.21.clone.four_ref), custom_call_target="tpu_custom_call" | custom-call | tf_op jit(solution)/shard_map/remain/pallas_call | solution.py:189
  185.9 53.8 %update.1 = f32[14336,128]{1,0:T(8,128)} custom-call(s32[448,256]{1,0:T(8,128)} %reshape_reshape.7.picked_ref, f32[448,256]{1,0:T(8,128)} %copy.22.value_ref, bf16[128,64]{1,0:T(8,128)(2,1)} %constant.20.clone.ct_ref, bf16[2,256,256]{2,1,0:T(8,128)(2,1)} %constant.21.clone.four_ref), custom_call_target="tpu_custom_call" | custom-call | tf_op jit(solution)/shard_map/update/pallas_call | solution.py:209
  239.7 0.0 all-to-all-done.2.g_ref
  239.7 11.2 %finish.1 = f32[896,2048]{1,0:T(8,128)} custom-call(f32[896,2048]{1,0:T(8,128)} %remain.1.a_ref, bf16[16,896,128]{2,1,0:T(8,128)(2,1)} %all-to-all-done.2.g_ref), custom_call_target="tpu_custom_call" | custom-call | tf_op jit(solution)/shard_map/finish/pallas_call | solution.py:234
  (5 shorter events, 0.1 us)
Async XLA Ops:
  3.9 24.2 %all-to-all-start = ((s32[16,1,7168]{2,1,0:T(1,128)}), s32[16,1,7168]{2,1,0:T(1,128)S(1)}, u32[]{:S(2)}, u32[]{:S(2)}) async-start(s32[16,1,7168]{2,1,0:T(1,128)} %reshape.88), calls=%async_computation | async-start | bytes 917504 | tf_op jit(solution)/shard_map/all_to_all | solution.py:262
  57.8 7.4 %copy-start.1 = (f32[112,128]{1,0:T(8,128)S(1)}, f32[112,128]{1,0:T(8,128)}, u32[]{:S(2)}) copy-start(f32[112,128]{1,0:T(8,128)} %values_tall.1) | copy-start | bytes 172036
  57.8 181.9 %all-to-all-start.2 = ((bf16[16,896,128]{2,1,0:T(8,128)(2,1)}), bf16[16,896,128]{2,1,0:T(8,128)(2,1)}, u32[]{:S(2)}, u32[]{:S(2)}) async-start(bf16[16,896,128]{2,1,0:T(8,128)(2,1)} %bitcast.22), calls=%async_computation.2 | async-start | bytes 7340032 | tf_op jit(solution)/shard_map/all_to_all | solution.py:267
  65.2 70.4 %copy-start = (f32[112,128]{1,0:T(8,128)S(1)}, f32[112,128]{1,0:T(8,128)}, u32[]{:S(2)}) copy-start(f32[112,128]{1,0:T(8,128)} %values_wide.1) | copy-start | bytes 172036

commit v2 on v0

v2 whole, which is shorter than its diff:
```python
import functools

import jax
import jax.numpy as jnp
import numpy as np
from jax import lax
from jax.experimental import pallas as pl
from jax.experimental.pallas import tpu as pltpu
from jax.sharding import PartitionSpec as P

SPAN = 64
TOPK = 32
DECAY = 0.999
LANES = 128
EARLY = 192
IN_KERNEL = 896

F32 = jnp.float32
BF16 = jnp.bfloat16
MESH = pl.DeviceIdType.MESH
ANY = pl.BlockSpec(memory_space=pl.ANY)
VMEM = pl.BlockSpec(memory_space=pltpu.VMEM)


def cosine_table():
    u = np.arange(SPAN, dtype=np.float64)[:, None]
    i = np.arange(SPAN, dtype=np.float64)[None, :]
    weight = np.where(u == 0, np.sqrt(1.0 / SPAN), np.sqrt(2.0 / SPAN))
    return weight * np.cos(np.pi * (2.0 * i + 1.0) * u / (2.0 * SPAN))


def two_parts(x):
    high = x.astype(jnp.bfloat16.dtype)
    low = (x - high.astype(np.float64)).astype(jnp.bfloat16.dtype)
    return high, low


def tables():
    c = cosine_table()
    turned = np.zeros((SPAN, LANES), np.float32)
    turned[:, :SPAN] = c.T
    owner = np.arange(LANES)[None, None, :] // TOPK == np.arange(4)[:, None, None]
    owner = np.broadcast_to(owner, (4, SPAN, LANES)).astype(jnp.bfloat16.dtype)
    return turned, owner, np.stack(two_parts(np.kron(np.eye(4), c)))


def split(x):
    high = x.astype(BF16)
    return high, (x - high.astype(F32)).astype(BF16)


def dot(a, b):
    return jnp.dot(a, b, preferred_element_type=F32)


def dot_nt(a, b):
    return lax.dot_general(a, b, (((1,), (1,)), ((), ())), preferred_element_type=F32)


def columns_of(table, row):
    where = jnp.broadcast_to(row, table.shape)
    return jnp.take_along_axis(table, where, axis=1, mode="promise_in_bounds")


def spread(part, owner_ref):
    return jnp.concatenate([part * owner_ref[q] for q in range(4)], axis=0)


def right_side(picked, turned, owner_ref):
    high, low = split(columns_of(turned, picked & 63))
    return jnp.concatenate([spread(high, owner_ref), spread(low, owner_ref)], axis=1)


def values_of(x, picked, turned, owner_ref):
    right = right_side(picked, turned, owner_ref)
    if x.dtype == BF16:
        z = dot(x, right)
        z = z[:, :LANES] + z[:, LANES:]
    else:
        z = dot(jnp.concatenate(split(x), axis=0), right)
        z = z[:SPAN, :LANES] + (z[:SPAN, LANES:] + z[SPAN:, :LANES] + z[SPAN:, LANES:])
    return jnp.sum(columns_of(turned, picked >> 6) * z, axis=0, keepdims=True)


def restored_of(picked, value, turned, owner_ref):
    high, low = split(columns_of(turned, picked >> 6) * value)
    left = jnp.concatenate(
        [jnp.concatenate([high, high], axis=1), jnp.concatenate([low, low], axis=1)], axis=0
    )
    r = dot_nt(left, right_side(picked, turned, owner_ref))
    return r[:SPAN] + r[SPAN:]


def pair(ref, j):
    top = ref[j * 128 : j * 128 + SPAN, :]
    return jnp.concatenate([top, ref[j * 128 + SPAN : (j + 1) * 128, :]], axis=1)


def exchange_kernel(
    gradient, momentum, picked, turned, owner,
    left, all_picked, all_value, arrived,
    mbuf, gbuf, col_picked, row_value, row_in, col_value, col_in, total,
    msem, gsem, lsem, osem, isend, irecv, rsend, rrecv, csend, crecv, asend, arecv, bsend, brecv,
    psend, precv,
    *, ways, replicas, early, rows_here,
):
    e = lax.axis_index("expert")
    r = lax.axis_index("dp")
    rows = mbuf.shape[1]
    units = rows // 128

    barrier = pltpu.get_barrier_semaphore()
    for d in range(1, ways):
        pl.semaphore_signal(barrier, inc=1, device_id={"expert": e ^ d}, device_id_type=MESH)
    for d in range(1, replicas):
        pl.semaphore_signal(barrier, inc=1, device_id={"dp": r ^ d}, device_id_type=MESH)

    def fetch_m(s):
        columns = pl.ds(pl.multiple_of(s * LANES, LANES), LANES)
        return pltpu.make_async_copy(momentum.at[:, columns], mbuf.at[s], msem.at[s])

    def fetch_g(s):
        here = pl.ds(pl.multiple_of(s * rows, 128), rows)
        return pltpu.make_async_copy(gradient.at[here], gbuf.at[s], gsem.at[s])

    @pl.loop(0, ways)
    def _(s):
        fetch_m(s).start()

    @pl.loop(0, ways)
    def _(s):
        fetch_g(s).start()

    pl.semaphore_wait(barrier, ways - 1 + replicas - 1)

    def to_expert(src, dst, send, recv, d):
        return pltpu.make_async_remote_copy(
            src_ref=src.at[e ^ d],
            dst_ref=dst.at[e],
            send_sem=send.at[d],
            recv_sem=recv.at[d],
            device_id={"expert": e ^ d},
            device_id_type=MESH,
        )

    def to_replica(src, dst, send, recv, d):
        return pltpu.make_async_remote_copy(
            src_ref=src,
            dst_ref=dst.at[r],
            send_sem=send.at[d],
            recv_sem=recv.at[d],
            device_id={"dp": r ^ d},
            device_id_type=MESH,
        )

    def bulk(d, part):
        start, size = ((0, early), (early, rows_here - early))[part]
        source = pl.ds(pl.multiple_of((e ^ d) * rows + start, 16), size)
        return pltpu.make_async_remote_copy(
            src_ref=gradient.at[source],
            dst_ref=arrived.at[e, pl.ds(start, size)],
            send_sem=bsend.at[part, d],
            recv_sem=brecv.at[part, d],
            device_id={"expert": e ^ d},
            device_id_type=MESH,
        )

    order = [d for d in range(1, ways) if d & 2] + [d for d in range(1, ways) if not d & 2]

    indices = [to_expert(picked, col_picked, isend, irecv, d) for d in order]
    for copy in indices:
        copy.start()
    first = [bulk(d, 0) for d in order]
    for copy in first:
        copy.start()
    col_picked[e] = picked[e]

    zero = jnp.zeros((1, LANES), F32)

    def values(out, source, where, fetch):
        @pl.loop(0, ways)
        def _(s):
            fetch(s).wait()
            found = [
                values_of(pair(source.at[s], j), where[s, j : j + 1, :], turned[...], owner)
                for j in range(units)
            ]
            out[s] = jnp.concatenate(found + [zero] * (8 - units), axis=0)

    values(row_value, mbuf, picked, fetch_m)
    rows_out = [to_expert(row_value, row_in, rsend, rrecv, d) for d in order]
    for copy in rows_out:
        copy.start()
    row_in[e] = row_value[e]

    for copy in indices:
        copy.wait()
    picked_out = [to_replica(col_picked, all_picked, asend, arecv, d) for d in range(1, replicas)]
    for copy in picked_out:
        copy.start()
    all_picked[r] = col_picked[...]

    values(col_value, gbuf, col_picked, fetch_g)
    cols_out = [to_expert(col_value, col_in, csend, crecv, d) for d in order]
    for copy in cols_out:
        copy.start()
    col_in[e] = col_value[e]

    for copy in rows_out:
        copy.wait()
    total[...] = DECAY * row_in[...] + col_value[...]
    value_out = [to_replica(total, all_value, psend, precv, d) for d in range(1, replicas)]
    for copy in value_out:
        copy.start()
    all_value[r] = total[...]

    own_slab = pltpu.make_async_copy(
        gbuf.at[e, pl.ds(0, rows_here)], arrived.at[e], lsem
    )
    own_slab.start()

    for copy in cols_out:
        copy.wait()
    second = [bulk(d, 1) for d in order] if rows_here > early else []
    for copy in second:
        copy.start()

    def back(s):
        return pltpu.make_async_copy(mbuf.at[s], left.at[s], osem.at[s])

    @pl.loop(0, ways)
    def _(s):
        value = DECAY * row_value[s] + col_in[s]
        for j in range(units):
            restored = restored_of(
                picked[s, j : j + 1, :], value[j : j + 1, :], turned[...], owner
            )
            for h in range(2):
                here = slice(j * 128 + h * SPAN, j * 128 + (h + 1) * SPAN)
                mbuf[s, here, :] = DECAY * mbuf[s, here, :] - restored[:, h * LANES : (h + 1) * LANES]
        back(s).start()

    @pl.loop(0, ways)
    def _(s):
        back(s).wait()

    own_slab.wait()
    for copy in picked_out + value_out + first + second:
        copy.wait()


def exchange(gradient, momentum, picked, turned, owner, ways, replicas):
    rows = momentum.shape[0]
    tile = (ways, 8, LANES)
    dma = pltpu.SemaphoreType.DMA
    return pl.pallas_call(
        functools.partial(
            exchange_kernel, ways=ways, replicas=replicas, early=EARLY, rows_here=IN_KERNEL
        ),
        in_specs=[ANY, ANY, VMEM, VMEM, VMEM],
        out_specs=[ANY, VMEM, VMEM, ANY],
        out_shape=[
            jax.ShapeDtypeStruct((ways, rows, LANES), F32),
            jax.ShapeDtypeStruct((replicas, *tile), jnp.int32),
            jax.ShapeDtypeStruct((replicas, *tile), F32),
            jax.ShapeDtypeStruct((ways, IN_KERNEL, LANES), BF16),
        ],
        scratch_shapes=[
            pltpu.VMEM((ways, rows, LANES), F32),
            pltpu.VMEM((ways, rows, LANES), BF16),
            pltpu.VMEM(tile, jnp.int32),
            *[pltpu.VMEM(tile, F32)] * 5,
            dma((ways,)),
            dma((ways,)),
            dma,
            dma((ways,)),
            *[dma((ways,))] * 6,
            *[dma((replicas,))] * 2,
            *[dma((2, ways))] * 2,
            *[dma((replicas,))] * 2,
        ],
        compiler_params=pltpu.CompilerParams(
            collective_id=0, has_side_effects=True, vmem_limit_bytes=24 << 20
        ),
        name="exchange",
    )(gradient, momentum, picked, turned, owner)


def update_kernel(picked_ref, value_ref, turned_ref, four_ref, out_hbm, th_ref, tl_ref, obuf, osem, *, units):
    steps = picked_ref.shape[0] // (4 * units)
    tall = units * 128
    rows = lax.broadcasted_iota(jnp.int32, (SPAN, 256), 0)

    def back(s):
        here = pl.ds(pl.multiple_of(s * tall, 128), tall)
        return pltpu.make_async_copy(obuf.at[here], out_hbm.at[here], osem.at[s])

    @pl.loop(0, steps)
    def _(s):
        for n in range(units):
            parts = []
            for b in range(4):
                k = (s * units + n) * 4 + b
                picked = picked_ref[pl.ds(k, 1), :]
                value = value_ref[pl.ds(k, 1), :]
                u = picked >> 6
                w = [columns_of(turned_ref[...], u[:, h * LANES : (h + 1) * LANES]) for h in range(2)]
                w = jnp.concatenate(w, axis=1) * value
                at_v = jnp.where(rows == (picked & 63), 1.0, 0.0).astype(BF16)
                t = dot_nt(jnp.concatenate(split(w), axis=0), at_v)
                parts.append(t[:SPAN] + t[SPAN:])
            high, low = split(jnp.concatenate(parts, axis=1))
            th_ref[n * SPAN : (n + 1) * SPAN, :] = high
            tl_ref[n * SPAN : (n + 1) * SPAN, :] = low
        r = dot(th_ref[...], four_ref[0]) + (dot(tl_ref[...], four_ref[0]) + dot(th_ref[...], four_ref[1]))
        for n in range(units):
            for h in range(2):
                here = pl.ds(pl.multiple_of(s * tall + n * 128 + h * SPAN, SPAN), SPAN)
                obuf[here, :] = r[n * SPAN : (n + 1) * SPAN, h * LANES : (h + 1) * LANES]
        back(s).start()

    @pl.loop(0, steps)
    def _(s):
        back(s).wait()


def update_of(picked, value, turned, four, units=8):
    blocks = picked.shape[0]
    rows = blocks * 32
    buf = pltpu.VMEM((units * SPAN, 256), BF16)
    return pl.pallas_call(
        functools.partial(update_kernel, units=units),
        in_specs=[VMEM] * 4,
        out_specs=ANY,
        out_shape=jax.ShapeDtypeStruct((rows, LANES), F32),
        scratch_shapes=[
            buf,
            buf,
            pltpu.VMEM((rows, LANES), F32),
            pltpu.SemaphoreType.DMA((blocks // (4 * units),)),
        ],
        compiler_params=pltpu.CompilerParams(vmem_limit_bytes=16 << 20),
        cost_estimate=pl.CostEstimate(flops=16_000_000_000, bytes_accessed=8_000_000, transcendentals=0),
        name="update",
    )(picked, value, turned, four)


def finish_kernel(left, *refs, starts):
    parts = len(starts)
    arrived, out, lbuf, gbuf, lsem, gsem, osem = refs[:parts], *refs[parts:]
    ways, rows = lbuf.shape[:2]

    def fetch(s):
        copies = [pltpu.make_async_copy(left.at[s], lbuf.at[s], lsem.at[s])]
        for n, (start, ref) in enumerate(zip(starts, arrived)):
            here = gbuf.at[s, pl.ds(start, ref.shape[1])]
            copies.append(pltpu.make_async_copy(ref.at[s], here, gsem.at[n, s]))
        return copies

    def back(s):
        columns = pl.ds(pl.multiple_of(s * LANES, LANES), LANES)
        return pltpu.make_async_copy(lbuf.at[s], out.at[:, columns], osem.at[s])

    @pl.loop(0, ways)
    def _(s):
        for copy in fetch(s):
            copy.start()

    @pl.loop(0, ways)
    def _(s):
        for copy in fetch(s):
            copy.wait()
        lbuf[s] = lbuf[s] + gbuf[s].astype(F32)
        back(s).start()

    @pl.loop(0, ways)
    def _(s):
        back(s).wait()


def finish(left, arrived):
    ways, rows, _ = left.shape
    starts = [sum(a.shape[1] for a in arrived[:n]) for n in range(len(arrived))]
    dma = pltpu.SemaphoreType.DMA
    return pl.pallas_call(
        functools.partial(finish_kernel, starts=tuple(starts)),
        in_specs=[ANY] * (1 + len(arrived)),
        out_specs=ANY,
        out_shape=jax.ShapeDtypeStruct((rows, ways * LANES), F32),
        scratch_shapes=[
            pltpu.VMEM(left.shape, F32),
            pltpu.VMEM(left.shape, BF16),
            dma((ways,)),
            dma((len(arrived), ways)),
            dma((ways,)),
        ],
        compiler_params=pltpu.CompilerParams(vmem_limit_bytes=16 << 20),
        name="finish",
    )(left, *arrived)


def on_device(gradient, momentum, group_index):
    turned, owner, four = (jnp.asarray(t) for t in tables())
    ways = lax.axis_size("expert")
    replicas = lax.axis_size("dp")
    total_rows = gradient.shape[2]
    rows, cols = momentum.shape[2:]
    units = rows // 128
    wide = cols // SPAN // ways

    gradient = gradient.reshape(total_rows, LANES)
    momentum = momentum.reshape(rows, cols)

    own = lax.dynamic_index_in_dim(group_index, lax.axis_index("dp"), 2, keepdims=False)
    own = own.reshape(units, 2, ways, wide, TOPK).transpose(2, 0, 1, 3, 4).reshape(ways, units, LANES)
    own = jnp.pad(own, ((0, 0), (0, 8 - units), (0, 0)))

    left, all_picked, all_value, arrived = exchange(
        gradient, momentum, own, turned, owner, ways, replicas
    )

    def by_block(x):
        x = x[:, :, :units].reshape(replicas, ways * units * 4, TOPK)
        return x.transpose(1, 0, 2).reshape(ways * units * 4, replicas * TOPK)

    pieces = [arrived]
    if IN_KERNEL < rows:
        gradient, all_value = lax.optimization_barrier((gradient, all_value))
        rest = gradient.reshape(ways, rows, LANES)[:, IN_KERNEL:]
        pieces.append(lax.all_to_all(rest, "expert", 0, 0, tiled=True))
    update = update_of(by_block(all_picked), by_block(all_value), turned, four)
    momentum_next = finish(left, pieces)
    return momentum_next.reshape(1, 1, rows, cols), update.reshape(1, total_rows, LANES)


def solution(mesh):
    return jax.shard_map(
        on_device,
        mesh=mesh,
        in_specs=(
            P("dp", None, None, "expert"),
            P("dp", None, "expert", None),
            P("expert", None, None, None),
        ),
        out_specs=(P("dp", None, "expert", None), P(None, None, "expert")),
        check_vma=False,
    )
```

time: 834 us -> 130 us (0.16); the launches traced: 818 us -> 129 us
  local copies, waits for them, and re-layouts: 321 us -> 20.2 us
  waiting for transfers between devices: 253 us -> 0 us
  other arithmetic: 128 us -> 0 us
  Pallas kernels: 0 us -> 108 us
  matrix products: 75.5 us -> 0 us
  starting transfers between devices: 26.2 us -> 0 us
  between operations: 14.6 us -> 0.72 us
    gather x2 -> x0, local copies, waits for them, and re-layouts: 200 us -> none  [on_device(): values = jnp.take_along_axis(coeffs, own, axis=2)]
    psum x1 -> x0, waiting for transfers between devices: 163 us -> none  [on_device(): total = lax.psum(restored, 'dp')]
    pallas_call x0 -> x3, Pallas kernels: none -> 108 us  [the longest x1 72.8 us: exchange(): pl.pallas_call(functools.partial(exchange_kernel, ways=ways, replicas=rep...]
    all_to_all x4 -> x0, waiting for transfers between devices: 89.3 us -> none  [several_exchanges(): lax.all_to_all(piece, axis, split_axis=0, concat_axis=0, tiled=True)]
    unnamed x5 -> x0, other arithmetic: 85.1 us -> none
    dot_general x4 -> x0, matrix products: 75.5 us -> none  [the longest x2 42.6 us: forward(): jnp.einsum('ui,piqj,vj->pquv', cosine, blocks, cosine, precision=HIGHEST_...]
    reshape x3 -> x6, local copies, waits for them, and re-layouts: 37.7 us -> 6.09 us  [the longest x2 3.32 us: by_block(): x = x[:, :, :units].reshape(replicas, ways * units * 4, TOPK)]
    all_to_all x4 -> x0, starting transfers between devices: 26.1 us -> none  [several_exchanges(): lax.all_to_all(piece, axis, split_axis=0, concat_axis=0, tiled=True)]
  transfers between devices with their start and end apart: 5 -> 0, of which waited for: 5 -> 0; matrix products, arithmetic and copies ran while one was open for 6% -> 0% of each run, Pallas kernels for 0% -> 0%
where the time goes in v2:
time: 130 us; the launch traced here: 129 us
  Pallas kernels  108 us (83%)
  local copies, waits for them, and re-layouts  20.2 us (16%)
    pallas_call x1, Pallas kernels, exchange(): pl.pallas_call(functools.partial(exchange_kernel, ways=ways, replicas=rep...  72.8 us
    pallas_call x1, Pallas kernels, update_of(): pl.pallas_call(functools.partial(update_kernel, units=units), in_specs=[V...  22.8 us
    pallas_call x1, Pallas kernels, finish(): pl.pallas_call(functools.partial(finish_kernel, starts=tuple(starts)), in...  12.6 us
    unnamed x14, local copies, waits for them, and re-layouts  8.21 us
    transpose x2, local copies, waits for them, and re-layouts, by_block(): return x.transpose(1, 0, 2).reshape(ways * units * 4, replicas * TOPK)  5.74 us
    reshape x2, local copies, waits for them, and re-layouts, by_block(): x = x[:, :, :units].reshape(replicas, ways * units * 4, TOPK)  3.32 us

profile of v2, /device:TPU:1, one launch (start us, length us, event | category | flops | bytes accessed | tf_op | source)
XLA Modules:
  0.0 129.2 jit_solution(14182410031354776026)
XLA Ops:
  0.6 0.0 copy-start
  0.6 1.5 %copy-done = s32[14,32,8,32]{3,2,1,0:T(8,128)S(1)} copy-done((s32[14,32,8,32]{3,2,1,0:T(8,128)S(1)}, s32[14,32,8,32]{3,2,1,0:T(8,128)}, u32[]{:S(2)}) %copy-start) | copy-done | bytes 458776
  2.1 0.2 constant_dynamic-slice_fusion
  2.3 0.1 copy.17
  2.4 0.2 reshape.45
  2.6 0.0 copy-start.1
  2.7 3.1 %copy-done.1 = f32[1,1,896,2048]{3,2,1,0:T(8,128)S(1)} copy-done((f32[1,1,896,2048]{3,2,1,0:T(8,128)S(1)}, f32[1,1,896,2048]{3,2,1,0:T(8,128)}, u32[]{:S(2)}) %copy-start.1) | copy-done | bytes 7340056
  5.7 0.0 copy-start.2
  5.7 2.0 %copy-done.2 = bf16[1,1,14336,128]{3,2,1,0:T(8,128)(2,1)S(1)} copy-done((bf16[1,1,14336,128]{3,2,1,0:T(8,128)(2,1)S(1)}, bf16[1,1,14336,128]{3,2,1,0:T(8,128)(2,1)}, u32[]{:S(2)}) %copy-start.2) | copy-done | bytes 3670040
  7.8 0.0 copy-start.3
  7.8 0.8 copy-done.3
  8.6 0.0 copy-start.4
  8.6 0.8 copy-done.4
  9.4 72.8 %exchange.1 = (f32[16,896,128]{2,1,0:T(8,128)S(1)}, s32[8,16,8,128]{3,2,1,0:T(8,128)S(1)}, f32[8,16,8,128]{3,2,1,0:T(8,128)S(1)}, bf16[16,896,128]{2,1,0:T(8,128)(2,1)S(1)}) custom-call(bf16[14336,128]{1,0:T(8,128)(2,1)S(1)} %bitcast.16, f32[896,2048]{1,0:T(8,128)S(1)} %bitcast.15, s32[16,8,128]{2,1,0:T(8,128)S(1)} %pad.4.picked, f32[64,128]{1,0:T(8,128)S(1)} %copy-done.4, ...), custom_call_target="tpu_custom_call" | custom-call | tf_op jit(solution)/shard_map/exchange/pallas_call | solution.py:256
  82.2 12.6 %finish.1 = f32[896,2048]{1,0:T(8,128)} custom-call(f32[16,896,128]{2,1,0:T(8,128)S(1)} %get-tuple-element.6.left, bf16[16,896,128]{2,1,0:T(8,128)(2,1)S(1)} %get-tuple-element.7.refs_0_), custom_call_target="tpu_custom_call" | custom-call | tf_op jit(solution)/shard_map/finish/pallas_call | solution.py:385
  94.8 1.7 %reshape.40 = s32[8,448,32]{2,1,0:T(8,128)} reshape(s32[8,16,7,128]{3,2,1,0:T(8,128)S(1)} %bitcast.18) | data formatting | bytes 917504 | tf_op jit(solution)/shard_map/reshape | solution.py:423
  96.5 2.9 %copy.13 = s32[448,8,32]{0,2,1:T(8,128)} copy(s32[448,8,32]{2,0,1:T(8,128)} %bitcast.20) | data formatting | bytes 917504 | tf_op jit(solution)/shard_map/transpose | solution.py:424
  99.3 0.0 copy-start.5
  99.3 0.0 copy-start.6
  99.3 1.3 copy.15.picked_ref
  100.6 1.7 %reshape.42 = f32[8,448,32]{2,1,0:T(8,128)} reshape(f32[8,16,7,128]{3,2,1,0:T(8,128)S(1)} %bitcast.17) | data formatting | bytes 917504 | tf_op jit(solution)/shard_map/reshape | solution.py:423
  102.3 2.9 %copy.14 = f32[448,8,32]{0,2,1:T(8,128)} copy(f32[448,8,32]{2,0,1:T(8,128)} %bitcast.21) | data formatting | bytes 917504 | tf_op jit(solution)/shard_map/transpose | solution.py:424
  105.1 1.2 copy.16.value_ref
  106.4 0.0 copy-done.5
  106.4 0.0 copy-done.6
  106.4 22.8 %update.1 = f32[14336,128]{1,0:T(8,128)} custom-call(s32[448,256]{1,0:T(8,128)S(1)} %copy.15.picked_ref, f32[448,256]{1,0:T(8,128)S(1)} %copy.16.value_ref, f32[64,128]{1,0:T(8,128)S(1)} %copy-done.5, bf16[2,256,256]{2,1,0:T(8,128)(2,1)S(1)} %copy-done.6), custom_call_target="tpu_custom_call" | custom-call | flops 16000000000 | bytes 8000000 | tf_op jit(solution)/shard_map/update/pallas_call | solution.py:331
  (1 shorter events, 0.0 us)
Async XLA Ops:
  0.6 1.5 %copy-start = (s32[14,32,8,32]{3,2,1,0:T(8,128)S(1)}, s32[14,32,8,32]{3,2,1,0:T(8,128)}, u32[]{:S(2)}) copy-start(s32[14,32,8,32]{3,2,1,0:T(8,128)} %param.8) | copy-start | bytes 1376260
  2.6 3.1 %copy-start.1 = (f32[1,1,896,2048]{3,2,1,0:T(8,128)S(1)}, f32[1,1,896,2048]{3,2,1,0:T(8,128)}, u32[]{:S(2)}) copy-start(f32[1,1,896,2048]{3,2,1,0:T(8,128)} %param.7) | copy-start | bytes 22020100
  5.7 2.0 %copy-start.2 = (bf16[1,1,14336,128]{3,2,1,0:T(8,128)(2,1)S(1)}, bf16[1,1,14336,128]{3,2,1,0:T(8,128)(2,1)}, u32[]{:S(2)}) copy-start(bf16[1,1,14336,128]{3,2,1,0:T(8,128)(2,1)} %param.6) | copy-start | bytes 11010052
  7.8 0.8 copy-start.3
  8.6 0.8 copy-start.4
  99.3 7.0 %copy-start.5 = (f32[64,128]{1,0:T(8,128)S(1)}, f32[64,128]{1,0:T(8,128)}, u32[]{:S(2)}) copy-start(f32[64,128]{1,0:T(8,128)} %constant.17.clone.turned.turned_ref) | copy-start | bytes 98308
  99.3 7.0 %copy-start.6 = (bf16[2,256,256]{2,1,0:T(8,128)(2,1)S(1)}, bf16[2,256,256]{2,1,0:T(8,128)(2,1)}, u32[]{:S(2)}) copy-start(bf16[2,256,256]{2,1,0:T(8,128)(2,1)} %constant.19.clone.four_ref) | copy-start | bytes 786436

commit v3 on v2

v3 whole, which is shorter than its diff:
```python
import functools

import jax
import jax.numpy as jnp
import numpy as np
from jax import lax
from jax.experimental import pallas as pl
from jax.experimental.pallas import tpu as pltpu
from jax.sharding import PartitionSpec as P

SPAN = 64
TOPK = 32
DECAY = 0.999
LANES = 128
CUTS = (0, 192, 320, 896)

F32 = jnp.float32
BF16 = jnp.bfloat16
MESH = pl.DeviceIdType.MESH
VMEM = pl.BlockSpec(memory_space=pltpu.VMEM)


def cosine_table():
    u = np.arange(SPAN, dtype=np.float64)[:, None]
    i = np.arange(SPAN, dtype=np.float64)[None, :]
    weight = np.where(u == 0, np.sqrt(1.0 / SPAN), np.sqrt(2.0 / SPAN))
    return weight * np.cos(np.pi * (2.0 * i + 1.0) * u / (2.0 * SPAN))


def two_parts(x):
    high = x.astype(jnp.bfloat16.dtype)
    low = (x - high.astype(np.float64)).astype(jnp.bfloat16.dtype)
    return high, low


def tables():
    c = cosine_table()
    turned = np.zeros((SPAN, LANES), np.float32)
    turned[:, :SPAN] = c.T
    return turned, np.stack(two_parts(np.kron(np.eye(4), c)))


def split(x):
    high = x.astype(BF16)
    return high, (x - high.astype(F32)).astype(BF16)


def dot(a, b):
    return jnp.dot(a, b, preferred_element_type=F32)


def dot_nt(a, b):
    return lax.dot_general(a, b, (((1,), (1,)), ((), ())), preferred_element_type=F32)


def columns_of(table, row):
    where = jnp.broadcast_to(row, table.shape)
    return jnp.take_along_axis(table, where, axis=1, mode="promise_in_bounds")


def spread(part, owner_ref):
    return jnp.concatenate([part * owner_ref[q] for q in range(4)], axis=0)


def right_side(picked, turned, owner_ref):
    high, low = split(columns_of(turned, picked & 63))
    return jnp.concatenate([spread(high, owner_ref), spread(low, owner_ref)], axis=1)


def values_of(x, picked, turned, owner_ref):
    right = right_side(picked, turned, owner_ref)
    if x.dtype == BF16:
        z = dot(x, right)
        z = z[:, :LANES] + z[:, LANES:]
    else:
        z = dot(jnp.concatenate(split(x), axis=0), right)
        z = z[:SPAN, :LANES] + (z[:SPAN, LANES:] + z[SPAN:, :LANES] + z[SPAN:, LANES:])
    return jnp.sum(columns_of(turned, picked >> 6) * z, axis=0, keepdims=True)


def restored_of(picked, value, turned, owner_ref):
    high, low = split(columns_of(turned, picked >> 6) * value)
    left = jnp.concatenate(
        [jnp.concatenate([high, high], axis=1), jnp.concatenate([low, low], axis=1)], axis=0
    )
    r = dot_nt(left, right_side(picked, turned, owner_ref))
    return r[:SPAN] + r[SPAN:]


def block_rows_of(found):
    replica = lax.broadcasted_iota(jnp.int32, (8, LANES), 0)
    group = lax.broadcasted_iota(jnp.int32, (8, LANES), 1) >> 5
    turned = found
    for n in range(1, 4):
        turned = jnp.where((replica & 3) == n, pltpu.roll(found, TOPK * n, 1), turned)
    rows = []
    for b in range(4):
        here = turned if b == 0 else pltpu.roll(turned, LANES - TOPK * b, 1)
        here = jnp.where((replica & 3) == group, here, jnp.zeros_like(here))
        here = here + pltpu.roll(here, 1, 0)
        here = here + pltpu.roll(here, 2, 0)
        rows.append((here[3:4], here[7:8]))
    return rows


def step_kernel(
    gradient, momentum, picked, turned_hbm, four_hbm,
    mn, update,
    gbuf, arrived, turned, owner, four, col_picked, row_value, row_in, col_value, col_in,
    all_picked, all_value, th, tl,
    msem, gsem, csem, isend, irecv, rsend, rrecv, csend, crecv, bsend, brecv,
    asend, arecv, psend, precv,
    *, ways, replicas, cuts,
):
    e = lax.axis_index("expert")
    r = lax.axis_index("dp")
    rows = gbuf.shape[1]
    units = rows // 128
    tiles = ways * 8

    barrier = pltpu.get_barrier_semaphore()
    for d in range(1, ways):
        pl.semaphore_signal(barrier, inc=1, device_id={"expert": e ^ d}, device_id_type=MESH)
    near = (1, 2, 3, 4)
    for d in near:
        pl.semaphore_signal(barrier, inc=1, device_id={"dp": r ^ d}, device_id_type=MESH)

    def columns(s):
        return pl.ds(pl.multiple_of(s * LANES, LANES), LANES)

    def fetch_m(s):
        return pltpu.make_async_copy(momentum.at[:, columns(s)], mn.at[:, columns(s)], msem.at[s])

    def fetch_g(s):
        here = pl.ds(pl.multiple_of(s * rows, 128), rows)
        return pltpu.make_async_copy(gradient.at[here], gbuf.at[s], gsem.at[s])

    constants = [
        pltpu.make_async_copy(turned_hbm, turned, csem.at[0]),
        pltpu.make_async_copy(four_hbm, four, csem.at[1]),
    ]
    constants[0].start()

    @pl.loop(0, ways)
    def _(s):
        fetch_m(s).start()

    @pl.loop(0, ways)
    def _(s):
        fetch_g(s).start()

    constants[1].start()
    lanes = lax.broadcasted_iota(jnp.int32, (SPAN, LANES), 1) >> 5
    for q in range(4):
        owner[q] = jnp.where(lanes == q, 1.0, 0.0).astype(BF16)

    pl.semaphore_wait(barrier, ways - 1 + len(near))

    def to_expert(src, dst, send, recv, d):
        return pltpu.make_async_remote_copy(
            src_ref=src.at[e ^ d],
            dst_ref=dst.at[e],
            send_sem=send.at[d],
            recv_sem=recv.at[d],
            device_id={"expert": e ^ d},
            device_id_type=MESH,
        )

    def to_replica(buf, slot, send, recv, d, n):
        here = pl.ds(pl.multiple_of(slot * tiles, 8), tiles)
        return pltpu.make_async_remote_copy(
            src_ref=buf.at[here],
            dst_ref=buf.at[here],
            send_sem=send.at[n],
            recv_sem=recv.at[n],
            device_id={"dp": r ^ d},
            device_id_type=MESH,
        )

    def bulk(d, part):
        start, size = cuts[part], cuts[part + 1] - cuts[part]
        source = pl.ds(pl.multiple_of((e ^ d) * rows + start, 16), size)
        return pltpu.make_async_remote_copy(
            src_ref=gradient.at[source],
            dst_ref=arrived.at[e, pl.ds(start, size)],
            send_sem=bsend.at[part, d],
            recv_sem=brecv.at[part, d],
            device_id={"expert": e ^ d},
            device_id_type=MESH,
        )

    order = [d for d in range(1, ways) if d & 2] + [d for d in range(1, ways) if not d & 2]

    def started(copies):
        for copy in copies:
            copy.start()
        return copies

    def waited(copies):
        for copy in copies:
            copy.wait()

    indices = started([to_expert(picked, col_picked, isend, irecv, d) for d in order])
    pieces = [started([bulk(d, 0) for d in order])]
    col_picked[e] = picked[e]
    constants[0].wait()

    zero = jnp.zeros((1, LANES), F32)

    def values(out, block_of, where, fetch, begin, end):
        @pl.loop(begin, end)
        def _(s):
            fetch(s).wait()
            found = [
                values_of(block_of(s, j), where[s, j : j + 1, :], turned[...], owner)
                for j in range(units)
            ]
            out[s] = jnp.concatenate(found + [zero] * (8 - units), axis=0)

    def halves(ref, j):
        return [slice(j * 128 + h * SPAN, j * 128 + (h + 1) * SPAN) for h in range(2)]

    def of_momentum(s, j):
        return jnp.concatenate([mn[here, columns(s)] for here in halves(mn, j)], axis=1)

    def of_gradient(s, j):
        return jnp.concatenate([gbuf[s, here, :] for here in halves(gbuf, j)], axis=1)

    values(row_value, of_momentum, picked, fetch_m, 0, ways)
    rows_out = started([to_expert(row_value, row_in, rsend, rrecv, d) for d in order])
    row_in[e] = row_value[e]

    waited(indices)
    mine = pl.ds(pl.multiple_of(r * tiles, 8), tiles)
    all_picked[mine, :] = col_picked[...].reshape(tiles, LANES)
    picked_out = started([to_replica(all_picked, r, asend, arecv, 4, 0)])
    pieces.append(started([bulk(d, 1) for d in order]))

    values(col_value, of_gradient, col_picked, fetch_g, 0, ways)
    cols_out = started([to_expert(col_value, col_in, csend, crecv, d) for d in order])
    col_in[e] = col_value[e]

    waited(rows_out)
    all_value[mine, :] = (DECAY * row_in[...] + col_value[...]).reshape(tiles, LANES)
    value_out = started([to_replica(all_value, r, psend, precv, 4, 0)])
    waited(picked_out)
    picked_out = []
    for n, d in enumerate((1, 2, 3)):
        for h in range(2):
            picked_out.append(to_replica(all_picked, r ^ (4 * h), asend, arecv, d, 1 + 2 * n + h))
    started(picked_out)
    pieces.append(started([bulk(d, 2) for d in order]))
    arrived[e] = gbuf[e]

    waited(cols_out)
    waited(value_out)
    value_out = []
    for n, d in enumerate((1, 2, 3)):
        for h in range(2):
            value_out.append(to_replica(all_value, r ^ (4 * h), psend, precv, d, 1 + 2 * n + h))
    started(value_out)

    @pl.loop(0, ways)
    def _(s):
        value = DECAY * row_value[s] + col_in[s]
        for j in range(units):
            restored = restored_of(
                picked[s, j : j + 1, :], value[j : j + 1, :], turned[...], owner
            )
            for h, here in enumerate(halves(mn, j)):
                mn[here, columns(s)] = (
                    DECAY * mn[here, columns(s)] - restored[:, h * LANES : (h + 1) * LANES]
                )

    constants[1].wait()
    waited(picked_out)
    waited(value_out)
    at = lax.broadcasted_iota(jnp.int32, (SPAN, 256), 0)

    @pl.loop(0, ways)
    def _(s):
        for j in range(units):
            each = pl.ds(s * 8 + j, replicas, stride=tiles)
            parts = []
            for index, value in zip(block_rows_of(all_picked[each, :]), block_rows_of(all_value[each, :])):
                w = [columns_of(turned[...], i >> 6) * v for i, v in zip(index, value)]
                v = jnp.concatenate(index, axis=1) & 63
                at_v = jnp.where(at == v, 1.0, 0.0).astype(BF16)
                t = dot_nt(jnp.concatenate(split(jnp.concatenate(w, axis=1)), axis=0), at_v)
                parts.append(t[:SPAN] + t[SPAN:])
            high, low = split(jnp.concatenate(parts, axis=1))
            th[j * SPAN : (j + 1) * SPAN, :] = high
            tl[j * SPAN : (j + 1) * SPAN, :] = low
        out = dot(th[...], four[0]) + (dot(tl[...], four[0]) + dot(th[...], four[1]))
        for j in range(units):
            for h in range(2):
                here = pl.ds(pl.multiple_of(s * rows + j * 128 + h * SPAN, SPAN), SPAN)
                update[here, :] = out[j * SPAN : (j + 1) * SPAN, h * LANES : (h + 1) * LANES]

    for d in [0] + order:
        if d:
            waited([piece[order.index(d)] for piece in pieces])
        source = e ^ d

        @pl.loop(0, units)
        def _(j):
            here = pl.ds(pl.multiple_of(j * 128, 128), 128)
            mn[here, columns(source)] = mn[here, columns(source)] + arrived[source, here, :].astype(F32)


def step(gradient, momentum, picked, turned, four, ways, replicas):
    rows = momentum.shape[0]
    tile = (ways, 8, LANES)
    dma = pltpu.SemaphoreType.DMA
    cuts = CUTS
    hbm = pl.BlockSpec(memory_space=pltpu.HBM)
    return pl.pallas_call(
        functools.partial(step_kernel, ways=ways, replicas=replicas, cuts=cuts),
        in_specs=[hbm, hbm, VMEM, hbm, hbm],
        out_specs=[VMEM, VMEM],
        out_shape=[
            jax.ShapeDtypeStruct(momentum.shape, F32),
            jax.ShapeDtypeStruct(gradient.shape, F32),
        ],
        scratch_shapes=[
            pltpu.VMEM((ways, rows, LANES), BF16),
            pltpu.VMEM((ways, rows, LANES), BF16),
            pltpu.VMEM(turned.shape, F32),
            pltpu.VMEM((4, SPAN, LANES), BF16),
            pltpu.VMEM(four.shape, BF16),
            pltpu.VMEM(tile, jnp.int32),
            *[pltpu.VMEM(tile, F32)] * 4,
            pltpu.VMEM((replicas * ways * 8, LANES), jnp.int32),
            pltpu.VMEM((replicas * ways * 8, LANES), F32),
            *[pltpu.VMEM((rows // 2, 256), BF16)] * 2,
            dma((ways,)),
            dma((ways,)),
            dma((2,)),
            *[dma((ways,))] * 6,
            *[dma((len(cuts) - 1, ways))] * 2,
            *[dma((7,))] * 4,
        ],
        compiler_params=pltpu.CompilerParams(
            collective_id=0, has_side_effects=True, vmem_limit_bytes=40 << 20
        ),
        name="step",
    )(gradient, momentum, picked, turned, four)


def on_device(gradient, momentum, group_index):
    turned, four = (jnp.asarray(t) for t in tables())
    ways = lax.axis_size("expert")
    replicas = lax.axis_size("dp")
    total_rows = gradient.shape[2]
    rows, cols = momentum.shape[2:]
    units = rows // 128
    wide = cols // SPAN // ways

    gradient = gradient.reshape(total_rows, LANES)
    momentum = momentum.reshape(rows, cols)

    own = lax.dynamic_index_in_dim(group_index, lax.axis_index("dp"), 2, keepdims=False)
    own = own.reshape(units, 2, ways, wide, TOPK).transpose(2, 0, 1, 3, 4).reshape(ways, units, LANES)
    own = jnp.pad(own, ((0, 0), (0, 8 - units), (0, 0)))

    momentum_next, update = step(gradient, momentum, own, turned, four, ways, replicas)
    return momentum_next.reshape(1, 1, rows, cols), update.reshape(1, total_rows, LANES)


def solution(mesh):
    return jax.shard_map(
        on_device,
        mesh=mesh,
        in_specs=(
            P("dp", None, None, "expert"),
            P("dp", None, "expert", None),
            P("expert", None, None, None),
        ),
        out_specs=(P("dp", None, "expert", None), P(None, None, "expert")),
        check_vma=False,
    )
```

time: 130 us -> 93.4 us (0.72)
  Pallas kernels: 108 us -> 77.9 us
  local copies, waits for them, and re-layouts: 20.2 us -> 14.5 us
    pallas_call x3 -> x1, Pallas kernels: 108 us -> 77.9 us  [step(): pl.pallas_call(functools.partial(step_kernel, ways=ways, replicas=replica...]
    reshape x4 -> x0, local copies, waits for them, and re-layouts: 5.8 us -> none  [the longest x2 3.32 us: by_block(): x = x[:, :, :units].reshape(replicas, ways * units * 4, TOPK)]
    unnamed x14 -> x12, local copies, waits for them, and re-layouts: 8.21 us -> 14 us
    transpose x2 -> x0, local copies, waits for them, and re-layouts: 5.74 us -> none  [by_block(): return x.transpose(1, 0, 2).reshape(ways * units * 4, replicas * TOPK)]
where the time goes in v3:
time: 93.4 us; the launch traced here: 93.1 us
  Pallas kernels  77.9 us (83%)
  local copies, waits for them, and re-layouts  14.5 us (16%)
    pallas_call x1, Pallas kernels, step(): pl.pallas_call(functools.partial(step_kernel, ways=ways, replicas=replica...  77.9 us
    unnamed x12, local copies, waits for them, and re-layouts  14 us

profile of v3, /device:TPU:1, one launch (start us, length us, event | category | flops | bytes accessed | tf_op | source)
XLA Modules:
  0.0 93.1 jit_solution(6068784042828511902)
XLA Ops:
  0.6 0.0 copy-start
  0.6 1.5 %copy-done = s32[14,32,8,32]{3,2,1,0:T(8,128)S(1)} copy-done((s32[14,32,8,32]{3,2,1,0:T(8,128)S(1)}, s32[14,32,8,32]{3,2,1,0:T(8,128)}, u32[]{:S(2)}) %copy-start) | copy-done | bytes 458776
  2.1 0.2 constant_dynamic-slice_fusion
  2.3 0.1 copy.10
  2.4 0.2 reshape.29
  2.6 0.0 copy-start.1
  2.7 2.0 %copy-done.1 = bf16[1,1,14336,128]{3,2,1,0:T(8,128)(2,1)S(1)} copy-done((bf16[1,1,14336,128]{3,2,1,0:T(8,128)(2,1)S(1)}, bf16[1,1,14336,128]{3,2,1,0:T(8,128)(2,1)}, u32[]{:S(2)}) %copy-start.1) | copy-done | bytes 3670040
  4.7 0.0 copy-start.2
  4.7 0.9 %copy-done.2 = bf16[2,256,256]{2,1,0:T(8,128)(2,1)S(1)} copy-done((bf16[2,256,256]{2,1,0:T(8,128)(2,1)S(1)}, bf16[2,256,256]{2,1,0:T(8,128)(2,1)}, u32[]{:S(2)}) %copy-start.2) | copy-done | bytes 262168
  5.6 0.0 copy-start.3
  5.6 0.8 copy-done.3
  6.4 77.9 %step.1 = (f32[896,2048]{1,0:T(8,128)S(1)}, f32[14336,128]{1,0:T(8,128)}) custom-call(bf16[14336,128]{1,0:T(8,128)(2,1)S(1)} %bitcast.10, f32[896,2048]{1,0:T(8,128)} %bitcast.12, s32[16,8,128]{2,1,0:T(8,128)S(1)} %pad.4.picked, f32[64,128]{1,0:T(8,128)S(1)} %copy-done.3, bf16[2,256,256]{2,1,0:T(8,128)(2,1)S(1)} %copy-done.2), custom_call_target="tpu_custom_call" | custom-call | tf_op jit(solution)/shard_map/step/pallas_call | solution.py:317
  84.3 0.0 copy-start.4
  84.3 3.7 %copy.15 = f32[1,1,896,2048]{3,2,1,0:T(8,128)} copy(f32[1,1,896,2048]{3,2,1,0:T(8,128)S(1)} %bitcast.9) | data formatting | bytes 14680064
  88.0 2.0 %copy-done.4 = f32[14336,128]{1,0:T(8,128)S(1)} copy-done((f32[14336,128]{1,0:T(8,128)S(1)}, f32[14336,128]{1,0:T(8,128)}, u32[]{:S(2)}) %copy-start.4) | copy-done | bytes 7340056
  90.0 3.0 %copy.16 = f32[1,14336,128]{2,1,0:T(8,128)} copy(f32[1,14336,128]{2,1,0:T(8,128)S(1)} %bitcast.11) | data formatting | bytes 14680064
  (1 shorter events, 0.0 us)
Async XLA Ops:
  0.6 1.5 %copy-start = (s32[14,32,8,32]{3,2,1,0:T(8,128)S(1)}, s32[14,32,8,32]{3,2,1,0:T(8,128)}, u32[]{:S(2)}) copy-start(s32[14,32,8,32]{3,2,1,0:T(8,128)} %param.7) | copy-start | bytes 1376260
  2.6 2.0 %copy-start.1 = (bf16[1,1,14336,128]{3,2,1,0:T(8,128)(2,1)S(1)}, bf16[1,1,14336,128]{3,2,1,0:T(8,128)(2,1)}, u32[]{:S(2)}) copy-start(bf16[1,1,14336,128]{3,2,1,0:T(8,128)(2,1)} %param.5) | copy-start | bytes 11010052
  4.7 0.9 %copy-start.2 = (bf16[2,256,256]{2,1,0:T(8,128)(2,1)S(1)}, bf16[2,256,256]{2,1,0:T(8,128)(2,1)}, u32[]{:S(2)}) copy-start(bf16[2,256,256]{2,1,0:T(8,128)(2,1)} %constant.16.clone.four_hbm) | copy-start | bytes 786436
  5.6 0.8 copy-start.3
  84.3 5.7 %copy-start.4 = (f32[14336,128]{1,0:T(8,128)S(1)}, f32[14336,128]{1,0:T(8,128)}, u32[]{:S(2)}) copy-start(f32[14336,128]{1,0:T(8,128)} %get-tuple-element.5) | copy-start | bytes 22020100

commit v4 on v3

--- a/solution.py
+++ b/solution.py
@@ -12,7 +12,9 @@
 TOPK = 32
 DECAY = 0.999
 LANES = 128
-CUTS = (0, 192, 320, 896)
+CUTS = (0, 128, 256, 896)
+PAIR = 2
+SPLIT = 14
 
 F32 = jnp.float32
 BF16 = jnp.bfloat16
@@ -103,14 +105,47 @@
     return rows
 
 
+def halves(j):
+    return [slice(j * 128 + h * SPAN, j * 128 + (h + 1) * SPAN) for h in range(2)]
+
+
+def sixteen(row):
+    return jnp.broadcast_to(row, (16, row.shape[1]))
+
+
+def decode(first, slabs, units, picked, value, turned, four, out, start, th, tl):
+    replicas = 8
+    stride = picked.shape[0] // replicas
+    at = (4, 16, 256)
+    at = lax.broadcasted_iota(jnp.int32, at, 0) * 16 + lax.broadcasted_iota(jnp.int32, at, 1)
+    at = at.astype(F32).astype(BF16)
+    one, none = jnp.ones(at.shape, BF16), jnp.zeros(at.shape, BF16)
+    for n in range(slabs * units):
+        each = pl.ds((first + n // units) * 8 + n % units, replicas, stride=stride)
+        parts = []
+        for index, val in zip(block_rows_of(picked[each, :]), block_rows_of(value[each, :])):
+            w = [columns_of(turned[...], i >> 6) * v for i, v in zip(index, val)]
+            v = sixteen((jnp.concatenate(index, axis=1) & 63).astype(F32)).astype(BF16)
+            at_v = jnp.where(at == v[None], one, none).reshape(SPAN, 256)
+            t = dot_nt(jnp.concatenate(split(jnp.concatenate(w, axis=1)), axis=0), at_v)
+            parts.append(t[:SPAN] + t[SPAN:])
+        high, low = split(jnp.concatenate(parts, axis=1))
+        th[n * SPAN : (n + 1) * SPAN, :] = high
+        tl[n * SPAN : (n + 1) * SPAN, :] = low
+    whole = dot(th[...], four[0]) + (dot(tl[...], four[0]) + dot(th[...], four[1]))
+    for n in range(slabs * units):
+        for h in range(2):
+            here = pl.ds(pl.multiple_of(start + n * 128 + h * SPAN, SPAN), SPAN)
+            out[here, :] = whole[n * SPAN : (n + 1) * SPAN, h * LANES : (h + 1) * LANES]
+
+
 def step_kernel(
     gradient, momentum, picked, turned_hbm, four_hbm,
-    mn, update,
-    gbuf, arrived, turned, owner, four, col_picked, row_value, row_in, col_value, col_in,
-    all_picked, all_value, th, tl,
+    mn, update, all_picked, all_value,
+    gbuf, arrived, turned, owner, four, col_picked, row_value, row_in, col_value, col_in, th, tl,
     msem, gsem, csem, isend, irecv, rsend, rrecv, csend, crecv, bsend, brecv,
     asend, arecv, psend, precv,
-    *, ways, replicas, cuts,
+    *, ways, cuts, slabs,
 ):
     e = lax.axis_index("expert")
     r = lax.axis_index("dp")
@@ -207,26 +242,30 @@
 
     zero = jnp.zeros((1, LANES), F32)
 
-    def values(out, block_of, where, fetch, begin, end):
-        @pl.loop(begin, end)
-        def _(s):
-            fetch(s).wait()
-            found = [
-                values_of(block_of(s, j), where[s, j : j + 1, :], turned[...], owner)
-                for j in range(units)
-            ]
-            out[s] = jnp.concatenate(found + [zero] * (8 - units), axis=0)
-
-    def halves(ref, j):
-        return [slice(j * 128 + h * SPAN, j * 128 + (h + 1) * SPAN) for h in range(2)]
+    def values(out, block_of, where, fetch):
+        @pl.loop(0, ways // PAIR)
+        def _(t):
+            for n in range(PAIR):
+                fetch(PAIR * t + n).wait()
+            for n in range(PAIR):
+                s = PAIR * t + n
+                found = [
+                    values_of(block_of(s, j), where[s, j : j + 1, :], turned[...], owner)
+                    for j in range(units)
+                ]
+                out[s] = jnp.concatenate(found + [zero] * (8 - units), axis=0)
 
     def of_momentum(s, j):
-        return jnp.concatenate([mn[here, columns(s)] for here in halves(mn, j)], axis=1)
+        blocks = []
+        for here in halves(j):
+            blocks.append(DECAY * mn[here, columns(s)])
+            mn[here, columns(s)] = blocks[-1]
+        return jnp.concatenate(blocks, axis=1)
 
     def of_gradient(s, j):
-        return jnp.concatenate([gbuf[s, here, :] for here in halves(gbuf, j)], axis=1)
-
-    values(row_value, of_momentum, picked, fetch_m, 0, ways)
+        return jnp.concatenate([gbuf[s, here, :] for here in halves(j)], axis=1)
+
+    values(row_value, of_momentum, picked, fetch_m)
     rows_out = started([to_expert(row_value, row_in, rsend, rrecv, d) for d in order])
     row_in[e] = row_value[e]
 
@@ -236,12 +275,12 @@
     picked_out = started([to_replica(all_picked, r, asend, arecv, 4, 0)])
     pieces.append(started([bulk(d, 1) for d in order]))
 
-    values(col_value, of_gradient, col_picked, fetch_g, 0, ways)
+    values(col_value, of_gradient, col_picked, fetch_g)
     cols_out = started([to_expert(col_value, col_in, csend, crecv, d) for d in order])
     col_in[e] = col_value[e]
 
     waited(rows_out)
-    all_value[mine, :] = (DECAY * row_in[...] + col_value[...]).reshape(tiles, LANES)
+    all_value[mine, :] = (row_in[...] + col_value[...]).reshape(tiles, LANES)
     value_out = started([to_replica(all_value, r, psend, precv, 4, 0)])
     waited(picked_out)
     picked_out = []
@@ -250,8 +289,26 @@
             picked_out.append(to_replica(all_picked, r ^ (4 * h), asend, arecv, d, 1 + 2 * n + h))
     started(picked_out)
     pieces.append(started([bulk(d, 2) for d in order]))
-    arrived[e] = gbuf[e]
-
+
+    def add_rows(source, s, start, size):
+        here = slice(start, start + size)
+        mn[here, columns(s)] = mn[here, columns(s)] + source[s, here, :].astype(F32)
+
+    def add_part(part):
+        def one(d):
+            bulk(d, part).wait()
+            add_rows(arrived, e ^ d, cuts[part], cuts[part + 1] - cuts[part])
+
+        @pl.loop(0, ways // 2)
+        def _(n):
+            one(4 * (n >> 1) + 2 + (n & 1))
+
+        @pl.loop(1, ways // 2)
+        def _(n):
+            one(4 * (n >> 1) + (n & 1))
+
+    add_rows(gbuf, e, 0, rows)
+    add_part(0)
     waited(cols_out)
     waited(value_out)
     value_out = []
@@ -260,67 +317,48 @@
             value_out.append(to_replica(all_value, r ^ (4 * h), psend, precv, d, 1 + 2 * n + h))
     started(value_out)
 
-    @pl.loop(0, ways)
-    def _(s):
-        value = DECAY * row_value[s] + col_in[s]
-        for j in range(units):
-            restored = restored_of(
-                picked[s, j : j + 1, :], value[j : j + 1, :], turned[...], owner
-            )
-            for h, here in enumerate(halves(mn, j)):
-                mn[here, columns(s)] = (
-                    DECAY * mn[here, columns(s)] - restored[:, h * LANES : (h + 1) * LANES]
+    @pl.loop(0, ways // PAIR)
+    def _(t):
+        for n in range(PAIR):
+            s = PAIR * t + n
+            value = row_value[s] + col_in[s]
+            for j in range(units):
+                restored = restored_of(
+                    picked[s, j : j + 1, :], value[j : j + 1, :], turned[...], owner
                 )
-
+                for h, here in enumerate(halves(j)):
+                    mn[here, columns(s)] = mn[here, columns(s)] - restored[:, h * LANES : (h + 1) * LANES]
+
+    add_part(1)
     constants[1].wait()
     waited(picked_out)
     waited(value_out)
-    at = lax.broadcasted_iota(jnp.int32, (SPAN, 256), 0)
-
-    @pl.loop(0, ways)
+
+    @pl.loop(0, slabs)
     def _(s):
-        for j in range(units):
-            each = pl.ds(s * 8 + j, replicas, stride=tiles)
-            parts = []
-            for index, value in zip(block_rows_of(all_picked[each, :]), block_rows_of(all_value[each, :])):
-                w = [columns_of(turned[...], i >> 6) * v for i, v in zip(index, value)]
-                v = jnp.concatenate(index, axis=1) & 63
-                at_v = jnp.where(at == v, 1.0, 0.0).astype(BF16)
-                t = dot_nt(jnp.concatenate(split(jnp.concatenate(w, axis=1)), axis=0), at_v)
-                parts.append(t[:SPAN] + t[SPAN:])
-            high, low = split(jnp.concatenate(parts, axis=1))
-            th[j * SPAN : (j + 1) * SPAN, :] = high
-            tl[j * SPAN : (j + 1) * SPAN, :] = low
-        out = dot(th[...], four[0]) + (dot(tl[...], four[0]) + dot(th[...], four[1]))
-        for j in range(units):
-            for h in range(2):
-                here = pl.ds(pl.multiple_of(s * rows + j * 128 + h * SPAN, SPAN), SPAN)
-                update[here, :] = out[j * SPAN : (j + 1) * SPAN, h * LANES : (h + 1) * LANES]
-
-    for d in [0] + order:
-        if d:
-            waited([piece[order.index(d)] for piece in pieces])
-        source = e ^ d
-
-        @pl.loop(0, units)
-        def _(j):
-            here = pl.ds(pl.multiple_of(j * 128, 128), 128)
-            mn[here, columns(source)] = mn[here, columns(source)] + arrived[source, here, :].astype(F32)
+        decode(s, 1, units, all_picked, all_value, turned, four, update, s * rows, th, tl)
+
+    add_part(2)
+
+
+def place(array):
+    return pltpu.with_memory_space_constraint(array, pltpu.HBM)
 
 
 def step(gradient, momentum, picked, turned, four, ways, replicas):
     rows = momentum.shape[0]
     tile = (ways, 8, LANES)
     dma = pltpu.SemaphoreType.DMA
-    cuts = CUTS
     hbm = pl.BlockSpec(memory_space=pltpu.HBM)
     return pl.pallas_call(
-        functools.partial(step_kernel, ways=ways, replicas=replicas, cuts=cuts),
+        functools.partial(step_kernel, ways=ways, cuts=CUTS, slabs=SPLIT),
         in_specs=[hbm, hbm, VMEM, hbm, hbm],
-        out_specs=[VMEM, VMEM],
+        out_specs=[VMEM] * 4,
         out_shape=[
             jax.ShapeDtypeStruct(momentum.shape, F32),
-            jax.ShapeDtypeStruct(gradient.shape, F32),
+            jax.ShapeDtypeStruct((SPLIT * rows, LANES), F32),
+            jax.ShapeDtypeStruct((replicas * ways * 8, LANES), jnp.int32),
+            jax.ShapeDtypeStruct((replicas * ways * 8, LANES), F32),
         ],
         scratch_shapes=[
             pltpu.VMEM((ways, rows, LANES), BF16),
@@ -330,25 +368,90 @@
             pltpu.VMEM(four.shape, BF16),
             pltpu.VMEM(tile, jnp.int32),
             *[pltpu.VMEM(tile, F32)] * 4,
-            pltpu.VMEM((replicas * ways * 8, LANES), jnp.int32),
-            pltpu.VMEM((replicas * ways * 8, LANES), F32),
             *[pltpu.VMEM((rows // 2, 256), BF16)] * 2,
             dma((ways,)),
             dma((ways,)),
             dma((2,)),
             *[dma((ways,))] * 6,
-            *[dma((len(cuts) - 1, ways))] * 2,
+            *[dma((len(CUTS) - 1, ways))] * 2,
             *[dma((7,))] * 4,
         ],
         compiler_params=pltpu.CompilerParams(
-            collective_id=0, has_side_effects=True, vmem_limit_bytes=40 << 20
+            collective_id=0, has_side_effects=True, vmem_limit_bytes=20 << 20
         ),
         name="step",
     )(gradient, momentum, picked, turned, four)
 
 
+def finish_kernel(
+    mn, update, all_picked, all_value, turned_hbm, four_hbm,
+    mn_out, update_out,
+    turned, four, tail, th, tl, csem, msem, usem,
+    *, ways,
+):
+    rows = mn.shape[0]
+    units = rows // 128
+    done = update.shape[0] // rows
+    constants = [
+        pltpu.make_async_copy(turned_hbm, turned, csem.at[0]),
+        pltpu.make_async_copy(four_hbm, four, csem.at[1]),
+    ]
+    for copy in constants:
+        copy.start()
+
+    def slab(s, n=1):
+        return pl.ds(s * rows, n * rows)
+
+    copies = [
+        pltpu.make_async_copy(update.at[slab(s)], update_out.at[slab(s)], usem.at[s]) for s in range(done)
+    ]
+    for j in range(units):
+        here = pl.ds(j * 128, 128)
+        copies.append(pltpu.make_async_copy(mn.at[here], mn_out.at[here], msem.at[j]))
+    for copy in copies:
+        copy.start()
+    for copy in constants:
+        copy.wait()
+
+    @pl.loop(done, ways)
+    def _(s):
+        decode(s, 1, units, all_picked, all_value, turned, four, tail, (s - done) * rows, th, tl)
+
+    for s in range(done, ways):
+        copies.append(pltpu.make_async_copy(tail.at[slab(s - done)], update_out.at[slab(s)], usem.at[s]))
+        copies[-1].start()
+    for copy in copies:
+        copy.wait()
+
+
+def finish(mn, update, all_picked, all_value, turned, four, ways):
+    rows = mn.shape[0]
+    dma = pltpu.SemaphoreType.DMA
+    hbm = pl.BlockSpec(memory_space=pltpu.HBM)
+    return pl.pallas_call(
+        functools.partial(finish_kernel, ways=ways),
+        in_specs=[VMEM] * 4 + [hbm] * 2,
+        out_specs=[hbm] * 2,
+        out_shape=[
+            jax.ShapeDtypeStruct(mn.shape, F32),
+            jax.ShapeDtypeStruct((ways * rows, LANES), F32),
+        ],
+        scratch_shapes=[
+            pltpu.VMEM(turned.shape, F32),
+            pltpu.VMEM(four.shape, BF16),
+            pltpu.VMEM(((ways - SPLIT) * rows, LANES), F32),
+            *[pltpu.VMEM((rows // 2, 256), BF16)] * 2,
+            dma((2,)),
+            dma((rows // 128,)),
+            dma((ways,)),
+        ],
+        compiler_params=pltpu.CompilerParams(vmem_limit_bytes=12 << 20),
+        name="finish",
+    )(mn, update, all_picked, all_value, turned, four)
+
+
 def on_device(gradient, momentum, group_index):
-    turned, four = (jnp.asarray(t) for t in tables())
+    turned, four = (place(jnp.asarray(t)) for t in tables())
     ways = lax.axis_size("expert")
     replicas = lax.axis_size("dp")
     total_rows = gradient.shape[2]
@@ -356,14 +459,15 @@
     units = rows // 128
     wide = cols // SPAN // ways
 
-    gradient = gradient.reshape(total_rows, LANES)
-    momentum = momentum.reshape(rows, cols)
+    gradient = place(gradient.reshape(total_rows, LANES))
+    momentum = place(momentum.reshape(rows, cols))
 
     own = lax.dynamic_index_in_dim(group_index, lax.axis_index("dp"), 2, keepdims=False)
     own = own.reshape(units, 2, ways, wide, TOPK).transpose(2, 0, 1, 3, 4).reshape(ways, units, LANES)
     own = jnp.pad(own, ((0, 0), (0, 8 - units), (0, 0)))
 
-    momentum_next, update = step(gradient, momentum, own, turned, four, ways, replicas)
+    parts = step(gradient, momentum, own, turned, four, ways, replicas)
+    momentum_next, update = finish(*parts, turned, four, ways)
     return momentum_next.reshape(1, 1, rows, cols), update.reshape(1, total_rows, LANES)
 
 

time: 93.4 us -> 72.5 us (0.78)
  local copies, waits for them, and re-layouts: 14.5 us -> 1.99 us
  Pallas kernels: 77.9 us -> 69.6 us
    unnamed x12 -> x2, local copies, waits for them, and re-layouts: 14 us -> 1.49 us
    pallas_call x1 -> x2, Pallas kernels: 77.9 us -> 69.6 us  [the longest x1 63.5 us: step(): pl.pallas_call(functools.partial(step_kernel, ways=ways, cuts=CUTS, slabs...]
where the time goes in v4:
time: 72.5 us; the launch traced here: 72.3 us
  Pallas kernels  69.6 us (96%)
  local copies, waits for them, and re-layouts  1.99 us (3%)
    pallas_call x1, Pallas kernels, step(): pl.pallas_call(functools.partial(step_kernel, ways=ways, cuts=CUTS, slabs...  63.5 us
    pallas_call x1, Pallas kernels, finish(): pl.pallas_call(functools.partial(finish_kernel, ways=ways), in_specs=[VME...  6.12 us
    unnamed x2, local copies, waits for them, and re-layouts  1.49 us

profile of v4, /device:TPU:1, one launch (start us, length us, event | category | flops | bytes accessed | tf_op | source)
XLA Modules:
  0.0 72.3 jit_solution(16306349944576538077)
XLA Ops:
  0.6 0.0 copy-start
  0.6 1.5 %copy-done = s32[14,32,8,32]{3,2,1,0:T(8,128)S(1)} copy-done((s32[14,32,8,32]{3,2,1,0:T(8,128)S(1)}, s32[14,32,8,32]{3,2,1,0:T(8,128)}, u32[]{:S(2)}) %copy-start) | copy-done | bytes 458776
  2.1 0.2 constant_dynamic-slice_fusion
  2.3 0.1 copy.10
  2.4 0.2 reshape.29
  2.6 63.5 %step.1 = (f32[896,2048]{1,0:T(8,128)S(1)}, f32[12544,128]{1,0:T(8,128)S(1)}, s32[1024,128]{1,0:T(8,128)S(1)}, f32[1024,128]{1,0:T(8,128)S(1)}) custom-call(bf16[14336,128]{1,0:T(8,128)(2,1)} %bitcast.10, f32[896,2048]{1,0:T(8,128)} %bitcast.9, s32[16,8,128]{2,1,0:T(8,128)S(1)} %pad.4.picked, f32[64,128]{1,0:T(8,128)} %constant.15.clone.turned_hbm, ...), custom_call_target="tpu_custom_call" | custom-call | tf_op jit(solution)/shard_map/step/pallas_call | solution.py:353
  66.1 6.1 %finish.1 = (f32[896,2048]{1,0:T(8,128)}, f32[14336,128]{1,0:T(8,128)}) custom-call(f32[896,2048]{1,0:T(8,128)S(1)} %get-tuple-element.8.mn, f32[12544,128]{1,0:T(8,128)S(1)} %get-tuple-element.9.update, s32[1024,128]{1,0:T(8,128)S(1)} %get-tuple-element.10.all_picked, f32[1024,128]{1,0:T(8,128)S(1)} %get-tuple-element.11.all_value, ...), custom_call_target="tpu_custom_call" | custom-call | tf_op jit(solution)/shard_map/finish/pallas_call | solution.py:431
  (1 shorter events, 0.0 us)
Async XLA Ops:
  0.6 1.5 %copy-start = (s32[14,32,8,32]{3,2,1,0:T(8,128)S(1)}, s32[14,32,8,32]{3,2,1,0:T(8,128)}, u32[]{:S(2)}) copy-start(s32[14,32,8,32]{3,2,1,0:T(8,128)} %param.7) | copy-start | bytes 1376260

commit v5 on v4

--- a/solution.py
+++ b/solution.py
@@ -272,7 +272,7 @@
     waited(indices)
     mine = pl.ds(pl.multiple_of(r * tiles, 8), tiles)
     all_picked[mine, :] = col_picked[...].reshape(tiles, LANES)
-    picked_out = started([to_replica(all_picked, r, asend, arecv, 4, 0)])
+    picked_out = started([to_replica(all_picked, r, asend, arecv, d, n) for n, d in enumerate((4, 1, 2, 3))])
     pieces.append(started([bulk(d, 1) for d in order]))
 
     values(col_value, of_gradient, col_picked, fetch_g)
@@ -281,13 +281,10 @@
 
     waited(rows_out)
     all_value[mine, :] = (row_in[...] + col_value[...]).reshape(tiles, LANES)
-    value_out = started([to_replica(all_value, r, psend, precv, 4, 0)])
-    waited(picked_out)
-    picked_out = []
-    for n, d in enumerate((1, 2, 3)):
-        for h in range(2):
-            picked_out.append(to_replica(all_picked, r ^ (4 * h), asend, arecv, d, 1 + 2 * n + h))
-    started(picked_out)
+    value_out = started([to_replica(all_value, r, psend, precv, d, n) for n, d in enumerate((4, 1, 2, 3))])
+    waited(picked_out[:1])
+    passed = [to_replica(all_picked, r ^ 4, asend, arecv, d, 3 + d) for d in (1, 2, 3)]
+    picked_out = picked_out[1:] + started(passed)
     pieces.append(started([bulk(d, 2) for d in order]))
 
     def add_rows(source, s, start, size):
@@ -309,13 +306,10 @@
 
     add_rows(gbuf, e, 0, rows)
     add_part(0)
+    waited(value_out[:1])
+    passed = [to_replica(all_value, r ^ 4, psend, precv, d, 3 + d) for d in (1, 2, 3)]
+    value_out = value_out[1:] + started(passed)
     waited(cols_out)
-    waited(value_out)
-    value_out = []
-    for n, d in enumerate((1, 2, 3)):
-        for h in range(2):
-            value_out.append(to_replica(all_value, r ^ (4 * h), psend, precv, d, 1 + 2 * n + h))
-    started(value_out)
 
     @pl.loop(0, ways // PAIR)
     def _(t):

time: 72.5 us -> 72.4 us (level)
  no operation moved by 1% of the time
where the time goes in v5:
time: 72.4 us; the launch traced here: 72.2 us
  Pallas kernels  69.6 us (96%)
  local copies, waits for them, and re-layouts  1.99 us (3%)
    pallas_call x1, Pallas kernels, step(): pl.pallas_call(functools.partial(step_kernel, ways=ways, cuts=CUTS, slabs...  63.4 us
    pallas_call x1, Pallas kernels, finish(): pl.pallas_call(functools.partial(finish_kernel, ways=ways), in_specs=[VME...  6.12 us
    unnamed x2, local copies, waits for them, and re-layouts  1.49 us

profile of v5, /device:TPU:1, one launch (start us, length us, event | category | flops | bytes accessed | tf_op | source)
XLA Modules:
  0.0 72.2 jit_solution(2297584994820876656)
XLA Ops:
  0.6 0.0 copy-start
  0.6 1.5 %copy-done = s32[14,32,8,32]{3,2,1,0:T(8,128)S(1)} copy-done((s32[14,32,8,32]{3,2,1,0:T(8,128)S(1)}, s32[14,32,8,32]{3,2,1,0:T(8,128)}, u32[]{:S(2)}) %copy-start) | copy-done | bytes 458776
  2.1 0.2 constant_dynamic-slice_fusion
  2.3 0.1 copy.10
  2.4 0.2 reshape.29
  2.6 63.4 %step.1 = (f32[896,2048]{1,0:T(8,128)S(1)}, f32[12544,128]{1,0:T(8,128)S(1)}, s32[1024,128]{1,0:T(8,128)S(1)}, f32[1024,128]{1,0:T(8,128)S(1)}) custom-call(bf16[14336,128]{1,0:T(8,128)(2,1)} %bitcast.10, f32[896,2048]{1,0:T(8,128)} %bitcast.9, s32[16,8,128]{2,1,0:T(8,128)S(1)} %pad.4.picked, f32[64,128]{1,0:T(8,128)} %constant.15.clone.turned_hbm, ...), custom_call_target="tpu_custom_call" | custom-call | tf_op jit(solution)/shard_map/step/pallas_call | solution.py:347
  66.1 6.1 %finish.1 = (f32[896,2048]{1,0:T(8,128)}, f32[14336,128]{1,0:T(8,128)}) custom-call(f32[896,2048]{1,0:T(8,128)S(1)} %get-tuple-element.8.mn, f32[12544,128]{1,0:T(8,128)S(1)} %get-tuple-element.9.update, s32[1024,128]{1,0:T(8,128)S(1)} %get-tuple-element.10.all_picked, f32[1024,128]{1,0:T(8,128)S(1)} %get-tuple-element.11.all_value, ...), custom_call_target="tpu_custom_call" | custom-call | tf_op jit(solution)/shard_map/finish/pallas_call | solution.py:425
  (1 shorter events, 0.0 us)
Async XLA Ops:
  0.6 1.5 %copy-start = (s32[14,32,8,32]{3,2,1,0:T(8,128)S(1)}, s32[14,32,8,32]{3,2,1,0:T(8,128)}, u32[]{:S(2)}) copy-start(s32[14,32,8,32]{3,2,1,0:T(8,128)} %param.7) | copy-start | bytes 1376260
